TPU v7x, 32 devices: a whole 2x2x4 slice. The times are simulated.
32 devices in a mesh: fsdp: 16 (over z, y, core), tp: 2 (over x).
Axes of the slice: x: 2, y: 2, z: 4, core: 2. Of those that a mesh axis runs over, the one named last changes fastest.
Arguments:
- hidden: bfloat16 [32, 5120], P(None, 'fsdp'), may hold values from -20 to 20
- query_weight: bfloat16 [5120, 5120], P(None, ('tp', 'fsdp')), may hold values from -0.078125 to 0.078125
- key_weight: bfloat16 [5120, 1024], P(None, ('tp', 'fsdp')), may hold values from -0.078125 to 0.078125
- value_weight: bfloat16 [5120, 1024], P(None, ('tp', 'fsdp')), may hold values from -0.078125 to 0.078125
- output_weight: bfloat16 [5120, 5120], P(('tp', 'fsdp')), may hold values from -0.078125 to 0.078125
- gate_weight: bfloat16 [5120, 27648], P(None, ('tp', 'fsdp')), may hold values from -0.078125 to 0.078125
- up_weight: bfloat16 [5120, 27648], P(None, ('tp', 'fsdp')), may hold values from -0.078125 to 0.078125
- down_weight: bfloat16 [27648, 5120], P(('tp', 'fsdp')), may hold values from -0.0390625 to 0.0390625
- history: float32 [7, 1024], replicated, may hold values from 0.0001 to 1, as said below
- slot: int32 [1], replicated, may hold values from 0 to 1023
- lengths: int32 [32], P('fsdp'), may hold values from 512 to 4096, as said below
- key_cache: bfloat16 [32, 4096, 1024], P('fsdp', None, 'tp'), may hold values from -1000 to 1000
- value_cache: bfloat16 [32, 4096, 1024], P('fsdp', None, 'tp'), may hold values from -6 to 6
Outputs:
- attention_out: bfloat16 [32, 5120], P('fsdp', 'tp')
- query_rollout: bfloat16 [5120, 5120], P('fsdp', 'tp')
- key_rollout: bfloat16 [5120, 1024], P('fsdp', 'tp')
- value_rollout: bfloat16 [5120, 1024], P('fsdp', 'tp')
- output_rollout: bfloat16 [5120, 5120], P('tp', 'fsdp')
- gate_rollout: bfloat16 [5120, 27648], P('fsdp', 'tp')
- up_rollout: bfloat16 [5120, 27648], P('fsdp', 'tp')
- down_rollout: bfloat16 [27648, 5120], P('tp', 'fsdp')
- new_history: float32 [7, 1024], replicated
Inputs may be any that keep to these rules, and one draw needn't show every extreme that they name: `history`: strictly positive. `lengths`: some sequence has all 4096 slots valid.
All inputs are finite; a program needn't handle non-finite values.
Results may differ from a plain program's by a relative error of at most 0.012.
The roundings to bfloat16 on the way count: a program that leaves them out, or rounds other values in their place, can miss the bound.
Values may be sent and summed in bfloat16 or wider, within the bound.
A program may use at most 192 MiB of HBM per device.

v0:
```python
import jax
import jax.numpy as jnp
from jax import lax
from jax.sharding import PartitionSpec as P

D = 5120
HEADS = 40
KV_HEADS = 8
HEAD_DIM = 128


target_peak = 4.0
norm_eps = 1e-06
rope_theta = 1000000.0


def largest(tensor):
    return jnp.max(jnp.abs(tensor.astype(jnp.float32)))


def scaling(peaks, history, slot):
    marked = lax.broadcasted_iota(jnp.int32, history.shape, 1) == slot[0]
    kept = jnp.max(jnp.where(marked, jnp.zeros_like(history), history), axis=1)
    return (target_peak / jnp.maximum(peaks, kept), jnp.where(marked, peaks[:, None], history))


def quantize(tensor, factor):
    return (tensor.astype(jnp.float32) * factor).astype(jnp.bfloat16)


def rotate(vectors, positions):
    half_dim = vectors.shape[-1] // 2
    ladder = jnp.arange(half_dim, dtype=jnp.float32)
    spread = rope_theta ** (-2.0 * ladder / vectors.shape[-1])
    angle = positions.astype(jnp.float32)[:, None] * spread[None, :]
    cosine = jnp.cos(angle)[:, None, :]
    sine = jnp.sin(angle)[:, None, :]
    first = vectors[..., :half_dim]
    second = vectors[..., half_dim:]
    return jnp.concatenate(
        [first * cosine - second * sine, second * cosine + first * sine], axis=-1
    )


def after(tensor, *earlier):
    return lax.optimization_barrier((tensor,) + earlier)[0]


def exchange_columns(part, *earlier):
    count = lax.axis_size("fsdp")
    rows, width = part.shape
    blocks = lax.optimization_barrier(part.reshape(count, rows // count, width))
    return lax.all_to_all(
        after(blocks, *earlier), "fsdp", split_axis=0, concat_axis=0, tiled=True
    )


def beside(blocks):
    count, rows, width = blocks.shape
    return blocks.transpose(1, 0, 2).reshape(rows, count * width)


def exchange_rows(part, *earlier):
    count = lax.axis_size("fsdp")
    rows, width = part.shape
    blocks = lax.optimization_barrier(
        part.reshape(rows, count, width // count).transpose(1, 0, 2)
    )
    return lax.all_to_all(
        after(blocks, *earlier), "fsdp", split_axis=0, concat_axis=0, tiled=True
    )


def below(blocks):
    count, rows, width = blocks.shape
    return blocks.reshape(count * rows, width)


def attend(query, key_new, value_new, key_cache, value_cache, lengths):
    count_seq = query.shape[0]
    kv_count = query.shape[1]
    head_dim = query.shape[3]
    cache_len = key_cache.shape[1]
    keys = key_cache.reshape(count_seq, cache_len, kv_count, head_dim)
    values = value_cache.reshape(count_seq, cache_len, kv_count, head_dim)
    scale = head_dim ** (-0.5)
    scores = jnp.einsum("bkgd,bjkd->bkgj", query, keys, preferred_element_type=jnp.float32) * scale
    own = (
        jnp.sum(query.astype(jnp.float32) * key_new.astype(jnp.float32)[:, :, None, :], axis=-1)
        * scale
    )
    valid = (lax.broadcasted_iota(jnp.int32, (count_seq, cache_len), 1) < lengths[:, None])[
        :, None, None, :
    ]
    top = jnp.maximum(jnp.max(jnp.where(valid, scores, -1e30), axis=-1), own)
    weights = jnp.where(valid, jnp.exp(scores - top[..., None]), 0.0)
    own_weight = jnp.exp(own - top)
    total = jnp.sum(weights, axis=-1) + own_weight
    probs = (weights / total[..., None]).astype(jnp.bfloat16)
    own_prob = (own_weight / total).astype(jnp.bfloat16)
    mixed = jnp.einsum("bkgj,bjkd->bkgd", probs, values, preferred_element_type=jnp.float32)
    mixed = (
        mixed
        + own_prob.astype(jnp.float32)[..., None] * value_new.astype(jnp.float32)[:, :, None, :]
    )
    return mixed.astype(jnp.bfloat16).reshape(count_seq, -1)


def per_device(
    hidden,
    query_weight,
    key_weight,
    value_weight,
    output_weight,
    gate_weight,
    up_weight,
    down_weight,
    history,
    slot,
    lengths,
    key_cache,
    value_cache,
):
    trainer = (
        query_weight,
        key_weight,
        value_weight,
        output_weight,
        gate_weight,
        up_weight,
        down_weight,
    )
    wide_q, wide_k = query_weight.shape[1], key_weight.shape[1]
    packed = exchange_columns(jnp.concatenate([query_weight, key_weight, value_weight], axis=1))
    local = after(jnp.stack([largest(tensor) for tensor in trainer]), packed)
    peaks = lax.pmax(local, ("fsdp", "tp"))
    factors, new_history = scaling(peaks, history, slot)
    gate_blocks = exchange_columns(gate_weight, peaks)
    query_rollout = quantize(beside(packed[:, :, :wide_q]), factors[0])
    key_rollout = quantize(beside(packed[:, :, wide_q : wide_q + wide_k]), factors[1])
    value_rollout = quantize(beside(packed[:, :, wide_q + wide_k :]), factors[2])
    widened = hidden.astype(jnp.float32)
    squares = jnp.sum(widened * widened, axis=1)
    joined = jnp.concatenate([query_rollout, key_rollout, value_rollout], axis=1)
    partial_value = jnp.dot(hidden, joined, preferred_element_type=jnp.float32)
    summed = lax.psum_scatter(
        jnp.concatenate([partial_value, squares[:, None]], axis=1),
        "fsdp",
        scatter_dimension=0,
        tiled=True,
    )
    up_blocks = exchange_columns(up_weight, gate_blocks, summed)
    gate_rollout = quantize(beside(gate_blocks), factors[4])
    total_sq = summed[:, -1]
    summed = summed[:, :-1]
    inv_rms = lax.rsqrt(total_sq / D + norm_eps)[:, None]
    width_q = query_rollout.shape[1]
    width_k = key_rollout.shape[1]
    query = summed[:, :width_q] * inv_rms / factors[0]
    key_new = summed[:, width_q : width_q + width_k] * inv_rms / factors[1]
    value_new = summed[:, width_q + width_k :] * inv_rms / factors[2]
    count_seq = summed.shape[0]
    query = rotate(query.reshape(count_seq, -1, HEAD_DIM), lengths).astype(jnp.bfloat16)
    query = query.reshape(count_seq, -1, HEADS // KV_HEADS, HEAD_DIM)
    key_new = rotate(key_new.reshape(count_seq, -1, HEAD_DIM), lengths).astype(jnp.bfloat16)
    value_new = value_new.reshape(count_seq, -1, HEAD_DIM).astype(jnp.bfloat16)
    attention_out = attend(query, key_new, value_new, key_cache, value_cache, lengths)
    down_arrived = exchange_rows(down_weight, up_blocks, gate_rollout, attention_out)
    up_rollout = quantize(beside(up_blocks), factors[5])
    output_arrived = exchange_rows(output_weight, down_arrived, up_rollout)
    down_rollout = quantize(below(down_arrived), factors[6])
    output_rollout = quantize(below(output_arrived), factors[3])
    return (
        attention_out,
        query_rollout,
        key_rollout,
        value_rollout,
        output_rollout,
        gate_rollout,
        up_rollout,
        down_rollout,
        new_history,
    )


def solution(mesh):
    return jax.shard_map(
        per_device,
        mesh=mesh,
        in_specs=(
            P(None, "fsdp"),
            P(None, ("tp", "fsdp")),
            P(None, ("tp", "fsdp")),
            P(None, ("tp", "fsdp")),
            P(("tp", "fsdp"), None),
            P(None, ("tp", "fsdp")),
            P(None, ("tp", "fsdp")),
            P(("tp", "fsdp"), None),
            P(),
            P(),
            P("fsdp"),
            P("fsdp", None, "tp"),
            P("fsdp", None, "tp"),
        ),
        out_specs=(
            P("fsdp", "tp"),
            P("fsdp", "tp"),
            P("fsdp", "tp"),
            P("fsdp", "tp"),
            P("tp", "fsdp"),
            P("fsdp", "tp"),
            P("fsdp", "tp"),
            P("tp", "fsdp"),
            P(),
        ),
        check_vma=False,
    )
```

profile of v0, /device:TPU:13, one launch (start us, length us, event | category | flops | bytes accessed | tf_op | source)
XLA Modules:
  0.0 907.3 jit_solution(2341549663295404438)
XLA Ops:
  18.6 6.5 all-to-all-start
  25.1 12.8 %copy.83 = bf16[5120,864]{1,0:T(8,128)(2,1)} copy(bf16[5120,864]{0,1:T(8,128)(2,1)} %param.18) | data formatting | bytes 17694720 | tf_op args[5]
  43.7 5.9 abs_reduce_fusion.2
  49.6 5.8 abs_reduce_fusion
  62.3 21.5 %all-to-all-done = bf16[16,320,224]{2,1,0:T(8,128)(2,1)S(1)} async-done(((bf16[16,320,224]{2,1,0:T(8,128)(2,1)}), bf16[16,320,224]{2,1,0:T(8,128)(2,1)S(1)}, u32[]{:S(2)}, u32[]{:S(2)}) %all-to-all-start) | async-done | bytes 2293792 | tf_op jit(solution)/shard_map/all_to_all | solution.py:53
  83.7 37.7 %pmax.7 = f32[7]{0:T(128)S(1)} all-reduce(f32[7]{0:T(128)S(1)} %stack.31), channel_id=1, replica_groups=mesh['fsdp'=16,'tp'=2] {'fsdp','tp'}, use_global_device_ids=true, to_apply=%region_7.0 | all-reduce | flops 7 | bytes 56 | tf_op jit(solution)/shard_map/pmax | solution.py:136
  121.4 7.5 all-to-all-start.1
  128.9 12.8 %copy.82 = bf16[5120,864]{1,0:T(8,128)(2,1)} copy(bf16[5120,864]{0,1:T(8,128)(2,1)} %param.19) | data formatting | bytes 17694720 | tf_op args[6]
  141.7 186.4 %all-to-all-done.1 = bf16[16,320,864]{2,1,0:T(8,128)(2,1)} async-done(((bf16[16,320,864]{2,1,0:T(8,128)(2,1)}), bf16[16,320,864]{2,1,0:T(8,128)(2,1)}, u32[]{:S(2)}, u32[]{:S(2)}) %all-to-all-start.1) | async-done | bytes 8847392 | tf_op jit(solution)/shard_map/all_to_all | solution.py:53
  353.0 12.7 %copy.81 = bf16[864,5120]{0,1:T(8,128)(2,1)} copy(bf16[864,5120]{1,0:T(8,128)(2,1)} %param.20) | data formatting | bytes 17694720 | tf_op args[7]
  367.0 216.1 %all-reduce.3.cloned.1.call-done = f32[32,3585]{1,0:T(8,128)} async-done(((f32[32,3585]{1,0:T(8,128)}), f32[32,3585]{1,0:T(8,128)}) %all-reduce.3.cloned.1.call-update) | async-done | bytes 458896
  588.3 5.8 select_reduce_fusion
  599.9 9.7 %fusion = bf16[320,16,864]{2,0,1:T(8,128)(2,1)} fusion(bf16[16,320,864]{2,1,0:T(8,128)(2,1)} %all-to-all-done.1, f32[]{:T(128)} %bitcast.26), kind=kLoop, calls=%fused_computation.6 | loop fusion | flops 13271040 | bytes 17694724 | tf_op jit(solution)/shard_map/convert_element_type | solution.py:28
  609.6 12.4 %copy.84 = bf16[320,16,864]{2,1,0:T(8,128)(2,1)} copy(bf16[320,16,864]{2,0,1:T(8,128)(2,1)} %fusion) | data formatting | bytes 17694720 | tf_op jit(solution)/shard_map/convert_element_type | solution.py:28
  622.0 16.1 %convert_element_type.206 = bf16[320,13824]{1,0:T(8,128)(2,1)} reshape(bf16[320,16,864]{2,1,0:T(8,128)(2,1)} %copy.84) | data formatting | bytes 17694720 | tf_op jit(solution)/shard_map/convert_element_type | solution.py:28
  638.2 7.2 all-to-all-start.3
  650.4 9.8 %fusion.1 = bf16[320,16,864]{2,0,1:T(8,128)(2,1)} fusion(bf16[16,320,864]{2,1,0:T(8,128)(2,1)} %all-to-all-done.2, f32[]{:T(128)} %bitcast.28), kind=kLoop, calls=%fused_computation.7 | loop fusion | flops 13271040 | bytes 17694724 | tf_op jit(solution)/shard_map/convert_element_type | solution.py:28
  660.2 12.4 %copy.85 = bf16[320,16,864]{2,1,0:T(8,128)(2,1)} copy(bf16[320,16,864]{2,0,1:T(8,128)(2,1)} %fusion.1) | data formatting | bytes 17694720 | tf_op jit(solution)/shard_map/convert_element_type | solution.py:28
  672.6 16.1 %convert_element_type.210 = bf16[320,13824]{1,0:T(8,128)(2,1)} reshape(bf16[320,16,864]{2,1,0:T(8,128)(2,1)} %copy.85) | data formatting | bytes 17694720 | tf_op jit(solution)/shard_map/convert_element_type | solution.py:28
  688.8 155.8 %all-to-all-done.3 = bf16[16,864,320]{1,2,0:T(8,128)(2,1)} async-done(((bf16[16,864,320]{1,2,0:T(8,128)(2,1)}), bf16[16,864,320]{1,2,0:T(8,128)(2,1)}, u32[]{:S(2)}, u32[]{:S(2)}) %all-to-all-start.3) | async-done | bytes 8847392 | tf_op jit(solution)/shard_map/all_to_all | solution.py:69
  844.6 5.1 all-to-all-start.4
  854.8 9.8 %multiply_convert_fusion = bf16[16,864,320]{1,2,0:T(8,128)(2,1)} fusion(bf16[16,864,320]{1,2,0:T(8,128)(2,1)} %all-to-all-done.3, f32[]{:T(128)} %bitcast.32), kind=kLoop, calls=%fused_computation | loop fusion | flops 13271040 | bytes 17694724 | tf_op jit(solution)/shard_map/convert_element_type | solution.py:28
  864.6 12.4 %copy.86 = bf16[16,864,320]{1,0,2:T(8,128)(2,1)} copy(bf16[16,864,320]{1,2,0:T(8,128)(2,1)} %multiply_convert_fusion) | data formatting | bytes 17694720 | tf_op jit(solution)/shard_map/convert_element_type | solution.py:28
  877.0 16.1 %convert_element_type.216 = bf16[13824,320]{0,1:T(8,128)(2,1)} reshape(bf16[16,864,320]{1,0,2:T(8,128)(2,1)} %copy.86) | data formatting | bytes 17694720 | tf_op jit(solution)/shard_map/convert_element_type | solution.py:28
  (79 shorter events, 76.8 us)
Async XLA Ops:
  18.6 65.2 %all-to-all-start = ((bf16[16,320,224]{2,1,0:T(8,128)(2,1)}), bf16[16,320,224]{2,1,0:T(8,128)(2,1)S(1)}, u32[]{:S(2)}, u32[]{:S(2)}) async-start(bf16[16,320,224]{2,1,0:T(8,128)(2,1)} %copy.69), calls=%async_computation | async-start | bytes 5242880 | tf_op jit(solution)/shard_map/all_to_all | solution.py:53
  25.1 12.8 %copy-start.1 = (bf16[5120,32]{0,1:T(8,128)(2,1)S(1)}, bf16[5120,32]{0,1:T(8,128)(2,1)}, u32[]{:S(2)}) copy-start(bf16[5120,32]{0,1:T(8,128)(2,1)} %param.16) | copy-start | bytes 983044
  25.1 13.4 %copy-start.2 = (bf16[5120,32]{0,1:T(8,128)(2,1)S(1)}, bf16[5120,32]{0,1:T(8,128)(2,1)}, u32[]{:S(2)}) copy-start(bf16[5120,32]{0,1:T(8,128)(2,1)} %param.15) | copy-start | bytes 983044
  43.6 11.8 %slice-start = ((s8[8847360]{0:T(1024)(128)(4,1)}), s8[4194304]{0:T(1024)(128)(4,1)S(1)}, s32[]{:S(2)}) async-start(s8[8847360]{0:T(1024)(128)(4,1)} %bitcast.74), calls=%async_computation.6 | async-start | bytes 8388608
  43.7 11.8 %slice-start.1 = ((s8[8847360]{0:T(1024)(128)(4,1)}), s8[4194304]{0:T(1024)(128)(4,1)S(1)}, s32[]{:S(2)}) async-start(s8[8847360]{0:T(1024)(128)(4,1)} %bitcast.74), calls=%async_computation.7 | async-start | bytes 8388608
  49.6 5.8 slice-start.2
  121.4 206.7 %all-to-all-start.1 = ((bf16[16,320,864]{2,1,0:T(8,128)(2,1)}), bf16[16,320,864]{2,1,0:T(8,128)(2,1)}, u32[]{:S(2)}, u32[]{:S(2)}) async-start(bf16[16,320,864]{2,1,0:T(8,128)(2,1)} %bitcast.73), calls=%async_computation.1 | async-start | bytes 18350080 | tf_op jit(solution)/shard_map/all_to_all | solution.py:53
  141.7 192.1 %copy-start.4 = (bf16[32,320]{1,0:T(8,128)(2,1)S(1)}, bf16[32,320]{1,0:T(8,128)(2,1)}, u32[]{:S(2)}) copy-start(bf16[32,320]{1,0:T(8,128)(2,1)} %param.13) | copy-start | bytes 61444
  141.7 192.3 %copy-start.5 = (s32[2]{0:T(128)S(1)}, s32[2]{0:T(128)}, u32[]{:S(2)}) copy-start(s32[2]{0:T(128)} %param.23) | copy-start | bytes 28
  141.7 192.4 %copy-start.3 = (f32[7,1024]{1,0:T(8,128)S(1)}, f32[7,1024]{1,0:T(8,128)}, u32[]{:S(2)}) copy-start(f32[7,1024]{1,0:T(8,128)} %param.21) | copy-start | bytes 86020
  328.1 310.0 %all-to-all-start.2 = ((bf16[16,320,864]{2,1,0:T(8,128)(2,1)}), bf16[16,320,864]{2,1,0:T(8,128)(2,1)}, u32[]{:S(2)}, u32[]{:S(2)}) async-start(bf16[16,320,864]{2,1,0:T(8,128)(2,1)} %bitcast.71), calls=%async_computation.2 | async-start | bytes 18350080 | tf_op jit(solution)/shard_map/all_to_all | solution.py:53
  332.9 250.2 %all-reduce.3.cloned.1.call-start = ((), (), s32[]{:S(2)}) async-start(), calls=%async_computation.5 | async-start | bytes 950272
  353.0 12.7 %copy-start.6 = (u32[32]{0:T(128)S(1)}, u32[32]{0:T(128)}, u32[]{:S(2)}) copy-start(u32[32]{0:T(128)} %constant.29) | copy-start | bytes 388
  638.2 206.4 %all-to-all-start.3 = ((bf16[16,864,320]{1,2,0:T(8,128)(2,1)}), bf16[16,864,320]{1,2,0:T(8,128)(2,1)}, u32[]{:S(2)}, u32[]{:S(2)}) async-start(bf16[16,864,320]{1,2,0:T(8,128)(2,1)} %bitcast.72), calls=%async_computation.3 | async-start | bytes 18350080 | tf_op jit(solution)/shard_map/all_to_all | solution.py:69
  688.8 161.9 %copy-start = (bf16[320,16,160]{0,2,1:T(8,128)(2,1)S(1)}, bf16[320,16,160]{0,2,1:T(8,128)(2,1)}, u32[]{:S(2)}) copy-start(bf16[320,16,160]{0,2,1:T(8,128)(2,1)} %copy.70) | copy-start | bytes 4915204
  844.6 49.7 %all-to-all-start.4 = ((bf16[16,160,320]{2,1,0:T(8,128)(2,1)}), bf16[16,160,320]{2,1,0:T(8,128)(2,1)}, u32[]{:S(2)}, u32[]{:S(2)}) async-start(bf16[16,160,320]{2,1,0:T(8,128)(2,1)} %bitcast.79), calls=%async_computation.4 | async-start | bytes 3932160 | tf_op jit(solution)/shard_map/all_to_all | solution.py:69
Sparse Core Ops, SparseCore 0:
  353.1 229.9 all-reduce.2
where the time goes:
time: 918 us; the launch traced here: 907 us
  waiting for transfers between devices  581 us (63%)
  local copies, waits for them, and re-layouts  160 us (17%)
  other arithmetic  68.6 us (7%)
  blocking collectives  37.7 us (4%)
  starting transfers between devices  31.4 us (3%)
  between operations  16 us (2%)
  matrix products  13 us (1%)
    unnamed x2, waiting for transfers between devices  216 us
    all_to_all x3, waiting for transfers between devices, exchange_columns(): lax.all_to_all(after(blocks, *earlier), 'fsdp', split_axis=0, concat_axis...  208 us
    all_to_all x2, waiting for transfers between devices, exchange_rows(): lax.all_to_all(after(blocks, *earlier), 'fsdp', split_axis=0, concat_axis...  157 us
    convert_element_type x9, local copies, waits for them, and re-layouts, quantize(): return (tensor.astype(jnp.float32) * factor).astype(jnp.bfloat16)  93.2 us
    unnamed x28, local copies, waits for them, and re-layouts  47.2 us
    convert_element_type x6, other arithmetic, quantize(): return (tensor.astype(jnp.float32) * factor).astype(jnp.bfloat16)  38.2 us
    pmax x1, blocking collectives, per_device(): peaks = lax.pmax(local, ('fsdp', 'tp'))  37.7 us
    reduce_max x7, other arithmetic, largest(): return jnp.max(jnp.abs(tensor.astype(jnp.float32)))  19.8 us
  transfers between devices with their start and end apart: 6, of which 5 were waited for; matrix products, arithmetic and copies ran while one was open for 25% of the time, Pallas kernels for 0%

commit v1 on v0

--- a/solution.py
+++ b/solution.py
@@ -1,12 +1,16 @@
+import functools
+import math
+
 import jax
 import jax.numpy as jnp
 from jax import lax
+from jax.experimental import pallas as pl
+from jax.experimental.pallas import tpu as pltpu
 from jax.sharding import PartitionSpec as P
 
-D = 5120
-HEADS = 40
-KV_HEADS = 8
 HEAD_DIM = 128
+LANES = 128
+SLAB = 16
 
 
 target_peak = 4.0
@@ -46,34 +50,281 @@
     return lax.optimization_barrier((tensor,) + earlier)[0]
 
 
-def exchange_columns(part, *earlier):
-    count = lax.axis_size("fsdp")
-    rows, width = part.shape
-    blocks = lax.optimization_barrier(part.reshape(count, rows // count, width))
+def exchange(blocks, *earlier):
     return lax.all_to_all(
         after(blocks, *earlier), "fsdp", split_axis=0, concat_axis=0, tiled=True
     )
 
 
-def beside(blocks):
-    count, rows, width = blocks.shape
-    return blocks.transpose(1, 0, 2).reshape(rows, count * width)
-
-
-def exchange_rows(part, *earlier):
-    count = lax.axis_size("fsdp")
-    rows, width = part.shape
-    blocks = lax.optimization_barrier(
-        part.reshape(rows, count, width // count).transpose(1, 0, 2)
-    )
-    return lax.all_to_all(
-        after(blocks, *earlier), "fsdp", split_axis=0, concat_axis=0, tiled=True
-    )
-
-
-def below(blocks):
-    count, rows, width = blocks.shape
-    return blocks.reshape(count * rows, width)
+def folds(width):
+    rest = width % LANES
+    return 1 if rest == 0 else LANES // math.gcd(rest, LANES)
+
+
+def tile_rows(rows, width):
+    return rows * width // LANES
+
+
+def lane_index(rows):
+    return lax.broadcasted_iota(jnp.int32, (rows, LANES), 1)
+
+
+def assemble(pieces):
+    total = sum(length for _, _, length in pieces)
+    lanes = lane_index(pieces[0][0].shape[0])
+    tiles = [None] * (total // LANES)
+    offset = 0
+    for value, start, length in pieces:
+        shift = (offset - start) % LANES
+        moved = pltpu.roll(value, shift, 1) if shift else value
+        for tile in range(offset // LANES, (offset + length - 1) // LANES + 1):
+            low = max(offset - tile * LANES, 0)
+            old = tiles[tile]
+            tiles[tile] = moved if low == 0 else jnp.where(lanes >= low, moved, old)
+        offset += length
+    return tiles
+
+
+def cost(count):
+    return pl.CostEstimate(flops=count, bytes_accessed=4 * count, transcendentals=0)
+
+
+def columns_fit(count, rows, width):
+    fold = folds(width)
+    return rows % (SLAB * fold) == 0 and count % folds(width) == 0 and width >= 1
+
+
+def rows_fit(count, rows, width):
+    return count % 2 == 0 and width > LANES and width % LANES == LANES // 2 and rows % (2 * SLAB) == 0
+
+
+def pack_columns_kernel(widths, rows, extra, *refs):
+    ins, extra_ref, out_ref, rest_ref = refs[: len(widths)], refs[-3], refs[-2], refs[-1]
+    total = sum(widths)
+    fold = folds(total)
+    full, rest = total // LANES, total % LANES
+    lead = widths[0]
+    assert full == lead // LANES
+    for tile in range(full):
+        out_ref[0, pl.ds(tile * rows, rows), :] = ins[0][:, tile * LANES : (tile + 1) * LANES]
+    if rest:
+        group = rows // fold
+        splits = [lead - full * LANES] + list(widths[1:])
+        for number, size in enumerate(splits):
+            first = full * LANES if number == 0 else 0
+            rest_ref[number, :, :size] = ins[number][:, first : first + size].astype(jnp.float32)
+
+        def step(index, carry):
+            pieces = []
+            for part in range(fold):
+                low = pl.multiple_of(part * group + index * SLAB, SLAB)
+                for number, size in enumerate(splits):
+                    pieces.append((rest_ref[number, pl.ds(low, SLAB), :], 0, size))
+            for tile, value in enumerate(assemble(pieces)):
+                low = pl.multiple_of(full * rows + tile * group + index * SLAB, SLAB)
+                out_ref[0, pl.ds(low, SLAB), :] = value.astype(jnp.bfloat16)
+            return carry
+
+        lax.fori_loop(0, group // SLAB, step, 0)
+    if extra:
+        out_ref[0, pl.ds(tile_rows(rows, total), extra), :] = extra_ref[0]
+
+
+def pack_columns(count, tensors, extra):
+    rows = tensors[0].shape[0] // count
+    widths = [tensor.shape[1] for tensor in tensors]
+    body = tile_rows(rows, sum(widths))
+    if not columns_fit(count, rows, sum(widths)):
+        joined = jnp.concatenate(tensors, axis=1) if len(tensors) > 1 else tensors[0]
+        flat = joined.reshape(count, -1, LANES)
+        return jnp.concatenate([flat, jnp.broadcast_to(extra, (count,) + extra.shape[1:])], axis=1)
+    extra_rows = extra.shape[1]
+    shared = extra.shape[0] == 1
+    return pl.pallas_call(
+        functools.partial(pack_columns_kernel, widths, rows, extra_rows),
+        grid=(count,),
+        in_specs=[pl.BlockSpec((rows, width), lambda f: (f, 0)) for width in widths]
+        + [
+            pl.BlockSpec(
+                (1, extra_rows, LANES), (lambda f: (0, 0, 0)) if shared else (lambda f: (f, 0, 0))
+            )
+        ],
+        out_specs=pl.BlockSpec((1, body + extra_rows, LANES), lambda f: (f, 0, 0)),
+        out_shape=jax.ShapeDtypeStruct((count, body + extra_rows, LANES), jnp.bfloat16),
+        scratch_shapes=[pltpu.VMEM((len(widths), rows, LANES), jnp.float32)],
+        cost_estimate=cost(count * body * LANES),
+    )(*tensors, extra)
+
+
+def pack_rows_kernel(rows, width, extra, in_ref, extra_ref, out_ref):
+    full, half = width // LANES, rows // 2
+    for side in range(2):
+        if side == 0:
+            for tile in range(full):
+                out_ref[0, pl.ds(tile * rows, rows), :] = in_ref[
+                    :, tile * LANES : (tile + 1) * LANES
+                ]
+
+        def step(index, carry):
+            lasts = []
+            for part in range(2):
+                low = pl.multiple_of(part * half + index * SLAB, SLAB)
+                values = [
+                    in_ref[pl.ds(low, SLAB), tile * LANES : (tile + 1) * LANES].astype(jnp.float32)
+                    for tile in range(side * full, side * full + full + 1)
+                ]
+                if side == 0:
+                    lasts.append((values[full], 0, LANES // 2))
+                else:
+                    pieces = [(values[0], LANES // 2, LANES // 2)]
+                    pieces += [(value, 0, LANES) for value in values[1:-1]]
+                    pieces += [(values[-1], 0, LANES // 2)]
+                    for tile, value in enumerate(assemble(pieces)):
+                        to = pl.multiple_of(tile * rows + part * half + index * SLAB, SLAB)
+                        out_ref[1, pl.ds(to, SLAB), :] = value.astype(jnp.bfloat16)
+                    lasts.append((values[-1], LANES // 2, LANES // 2))
+            to = pl.multiple_of(full * rows + index * SLAB, SLAB)
+            out_ref[side, pl.ds(to, SLAB), :] = assemble(lasts)[0].astype(jnp.bfloat16)
+            return carry
+
+        lax.fori_loop(0, half // SLAB, step, 0)
+        if extra:
+            out_ref[side, pl.ds(tile_rows(rows, width), extra), :] = extra_ref[0]
+
+
+def pack_rows(count, tensor, extra):
+    rows = tensor.shape[0]
+    width = tensor.shape[1] // count
+    body = tile_rows(rows, width)
+    extra_rows = extra.shape[1]
+    if not rows_fit(count, rows, width):
+        flat = tensor.reshape(rows, count, width).transpose(1, 0, 2).reshape(count, -1, LANES)
+        return jnp.concatenate([flat, jnp.broadcast_to(extra, (count,) + extra.shape[1:])], axis=1)
+    return pl.pallas_call(
+        functools.partial(pack_rows_kernel, rows, width, extra_rows),
+        grid=(count // 2,),
+        in_specs=[
+            pl.BlockSpec((rows, 2 * width), lambda f: (0, f)),
+            pl.BlockSpec((1, extra_rows, LANES), lambda f: (0, 0, 0)),
+        ],
+        out_specs=pl.BlockSpec((2, body + extra_rows, LANES), lambda f: (f, 0, 0)),
+        out_shape=jax.ShapeDtypeStruct((count, body + extra_rows, LANES), jnp.bfloat16),
+        cost_estimate=cost(count * body * LANES),
+    )(tensor, extra)
+
+
+def unpack_columns_kernel(widths, numbers, rows, factor_ref, in_ref, *out_refs):
+    total = sum(widths)
+    fold = folds(total)
+    group = rows // fold
+    full, rest = total // LANES, total % LANES
+    sources = in_ref.shape[0]
+    for part in range(fold):
+
+        def step(index, carry):
+            pieces = [[] for _ in widths]
+            low = pl.multiple_of(part * group + index * SLAB, SLAB)
+            for source in range(sources):
+                have = []
+                for tile in range(full):
+                    at = pl.multiple_of(tile * rows + part * group + index * SLAB, SLAB)
+                    have.append((in_ref[source, pl.ds(at, SLAB), :].astype(jnp.float32), 0, LANES))
+                first = part * rest
+                while first < (part + 1) * rest:
+                    tile = first // LANES
+                    last = min((part + 1) * rest, (tile + 1) * LANES)
+                    at = pl.multiple_of(full * rows + tile * group + index * SLAB, SLAB)
+                    value = in_ref[source, pl.ds(at, SLAB), :].astype(jnp.float32)
+                    have.append((value, first - tile * LANES, last - first))
+                    first = last
+                for number, width in enumerate(widths):
+                    need = width
+                    while need:
+                        value, start, length = have.pop(0)
+                        taken = min(need, length)
+                        pieces[number].append((value, start, taken))
+                        if taken < length:
+                            have.insert(0, (value, start + taken, length - taken))
+                        need -= taken
+            for number, out_ref in enumerate(out_refs):
+                factor = factor_ref[numbers[number]]
+                for tile, value in enumerate(assemble(pieces[number])):
+                    out_ref[pl.ds(low, SLAB), tile * LANES : (tile + 1) * LANES] = (
+                        value * factor
+                    ).astype(jnp.bfloat16)
+            return carry
+
+        lax.fori_loop(0, group // SLAB, step, 0)
+
+
+def unpack_columns(count, arrived, rows, widths, factors, numbers):
+    total = sum(widths)
+    body = tile_rows(rows, total)
+    if not columns_fit(count, rows, total):
+        blocks = arrived[:, :body].reshape(count, rows, total)
+        outs, low = [], 0
+        for width, number in zip(widths, numbers):
+            part = blocks[:, :, low : low + width].transpose(1, 0, 2).reshape(rows, count * width)
+            outs.append(quantize(part, factors[number]))
+            low += width
+        return tuple(outs)
+    sources = max(folds(width) for width in widths)
+    return pl.pallas_call(
+        functools.partial(unpack_columns_kernel, widths, numbers, rows),
+        grid=(count // sources,),
+        in_specs=[
+            pl.BlockSpec(memory_space=pltpu.SMEM),
+            pl.BlockSpec((sources, body, LANES), lambda g: (g, 0, 0)),
+        ],
+        out_specs=[pl.BlockSpec((rows, sources * width), lambda g: (0, g)) for width in widths],
+        out_shape=[jax.ShapeDtypeStruct((rows, count * width), jnp.bfloat16) for width in widths],
+        cost_estimate=cost(count * body * LANES),
+    )(factors, arrived)
+
+
+def unpack_rows_kernel(number, rows, width, factor_ref, in_ref, out_ref):
+    full, half = width // LANES, rows // 2
+    factor = factor_ref[number]
+    for tile in range(full):
+        value = in_ref[0, pl.ds(tile * rows, rows), :].astype(jnp.float32)
+        out_ref[:, tile * LANES : (tile + 1) * LANES] = (value * factor).astype(jnp.bfloat16)
+    last = in_ref[0, pl.ds(full * rows, half), :].astype(jnp.float32) * factor
+    out_ref[pl.ds(0, half), full * LANES :] = last[:, : LANES // 2].astype(jnp.bfloat16)
+    turned = pltpu.roll(last, LANES // 2, 1)
+    out_ref[pl.ds(half, half), full * LANES :] = turned[:, : LANES // 2].astype(jnp.bfloat16)
+
+
+def unpack_rows(count, arrived, rows, width, factors, number):
+    body = tile_rows(rows, width)
+    if not rows_fit(count, rows, width):
+        return quantize(arrived[:, :body].reshape(count * rows, width), factors[number])
+    return pl.pallas_call(
+        functools.partial(unpack_rows_kernel, number, rows, width),
+        grid=(count,),
+        in_specs=[
+            pl.BlockSpec(memory_space=pltpu.SMEM),
+            pl.BlockSpec((1, body, LANES), lambda s: (s, 0, 0)),
+        ],
+        out_specs=pl.BlockSpec((rows, width), lambda s: (s, 0)),
+        out_shape=jax.ShapeDtypeStruct((count * rows, width), jnp.bfloat16),
+        cost_estimate=cost(count * body * LANES),
+    )(factors, arrived)
+
+
+def padded_rows(values, multiple):
+    lead, size = values.shape
+    unit = multiple * LANES
+    room = -(-size // unit) * unit
+    return jnp.pad(values, ((0, 0), (0, room - size))).reshape(lead, room // LANES, LANES)
+
+
+def split_float(values):
+    parts = []
+    for _ in range(3):
+        part = lax.reduce_precision(values, 8, 7)
+        parts.append(part.astype(jnp.bfloat16))
+        values = values - part
+    return jnp.stack(parts)
 
 
 def attend(query, key_new, value_new, key_cache, value_cache, lengths):
@@ -130,46 +381,71 @@
         up_weight,
         down_weight,
     )
-    wide_q, wide_k = query_weight.shape[1], key_weight.shape[1]
-    packed = exchange_columns(jnp.concatenate([query_weight, key_weight, value_weight], axis=1))
-    local = after(jnp.stack([largest(tensor) for tensor in trainer]), packed)
-    peaks = lax.pmax(local, ("fsdp", "tp"))
+    count = lax.axis_size("fsdp")
+    model = query_weight.shape[0]
+    rows = model // count
+    seqs = hidden.shape[0]
+    mine = lengths.shape[0]
+    widths = [query_weight.shape[1], key_weight.shape[1], value_weight.shape[1]]
+    group = query_weight.shape[1] // key_weight.shape[1]
+
+    sent_hidden = hidden.reshape(1, -1, LANES)
+    first = exchange(pack_rows(count, output_weight, sent_hidden))
+    local = jnp.stack([largest(tensor) for tensor in trainer])
+    sent_local = padded_rows(local[None, :].astype(jnp.bfloat16), SLAB)
+    second = exchange(pack_columns(count, trainer[:3], sent_local), first)
+    none = jnp.zeros((1, SLAB, LANES), jnp.bfloat16)
+    third = exchange(pack_columns(count, (gate_weight,), none), second)
+
+    body = tile_rows(rows, sum(widths))
+    heard = second[:, body:].reshape(count, -1)[:, :7].astype(jnp.float32)
+    peaks = lax.pmax(jnp.max(heard, axis=0), "tp")
     factors, new_history = scaling(peaks, history, slot)
-    gate_blocks = exchange_columns(gate_weight, peaks)
-    query_rollout = quantize(beside(packed[:, :, :wide_q]), factors[0])
-    key_rollout = quantize(beside(packed[:, :, wide_q : wide_q + wide_k]), factors[1])
-    value_rollout = quantize(beside(packed[:, :, wide_q + wide_k :]), factors[2])
-    widened = hidden.astype(jnp.float32)
-    squares = jnp.sum(widened * widened, axis=1)
-    joined = jnp.concatenate([query_rollout, key_rollout, value_rollout], axis=1)
-    partial_value = jnp.dot(hidden, joined, preferred_element_type=jnp.float32)
-    summed = lax.psum_scatter(
-        jnp.concatenate([partial_value, squares[:, None]], axis=1),
-        "fsdp",
-        scatter_dimension=0,
-        tiled=True,
-    )
-    up_blocks = exchange_columns(up_weight, gate_blocks, summed)
-    gate_rollout = quantize(beside(gate_blocks), factors[4])
-    total_sq = summed[:, -1]
-    summed = summed[:, :-1]
-    inv_rms = lax.rsqrt(total_sq / D + norm_eps)[:, None]
-    width_q = query_rollout.shape[1]
-    width_k = key_rollout.shape[1]
-    query = summed[:, :width_q] * inv_rms / factors[0]
-    key_new = summed[:, width_q : width_q + width_k] * inv_rms / factors[1]
-    value_new = summed[:, width_q + width_k :] * inv_rms / factors[2]
-    count_seq = summed.shape[0]
-    query = rotate(query.reshape(count_seq, -1, HEAD_DIM), lengths).astype(jnp.bfloat16)
-    query = query.reshape(count_seq, -1, HEADS // KV_HEADS, HEAD_DIM)
-    key_new = rotate(key_new.reshape(count_seq, -1, HEAD_DIM), lengths).astype(jnp.bfloat16)
-    value_new = value_new.reshape(count_seq, -1, HEAD_DIM).astype(jnp.bfloat16)
-    attention_out = attend(query, key_new, value_new, key_cache, value_cache, lengths)
-    down_arrived = exchange_rows(down_weight, up_blocks, gate_rollout, attention_out)
-    up_rollout = quantize(beside(up_blocks), factors[5])
-    output_arrived = exchange_rows(output_weight, down_arrived, up_rollout)
-    down_rollout = quantize(below(down_arrived), factors[6])
-    output_rollout = quantize(below(output_arrived), factors[3])
+    body = tile_rows(output_weight.shape[0], rows)
+    whole_hidden = first[:, body:].reshape(count, seqs, rows).transpose(1, 0, 2)
+    whole_hidden = whole_hidden.reshape(seqs, model)
+    widened = whole_hidden.astype(jnp.float32)
+    inv_rms = lax.rsqrt(jnp.mean(widened * widened, axis=1) + norm_eps)[:, None]
+    fresh = jnp.concatenate(
+        [
+            jnp.dot(
+                whole_hidden,
+                quantize(trainer[number], factors[number]),
+                preferred_element_type=jnp.float32,
+            )
+            * inv_rms
+            / factors[number]
+            for number in range(3)
+        ],
+        axis=1,
+    )
+    pieces = split_float(fresh).reshape(3, count, mine, -1).transpose(1, 0, 2, 3)
+    sent_fresh = padded_rows(pieces.reshape(count, -1), SLAB)
+    fourth = exchange(pack_columns(count, (up_weight,), sent_fresh), third)
+    fifth = exchange(pack_columns(count, (down_weight.T,), none), fourth)
+
+    query_rollout, key_rollout, value_rollout = unpack_columns(
+        count, second, rows, widths, factors, (0, 1, 2)
+    )
+    output_rollout = unpack_rows(count, first, output_weight.shape[0], rows, factors, 3)
+    (gate_rollout,) = unpack_columns(count, third, rows, [gate_weight.shape[1]], factors, (4,))
+    (up_rollout,) = unpack_columns(count, fourth, rows, [up_weight.shape[1]], factors, (5,))
+    (down_rollout,) = unpack_columns(count, fifth, rows, [down_weight.shape[0]], factors, (6,))
+    down_rollout = down_rollout.T
+
+    body = tile_rows(rows, up_weight.shape[1])
+    heard = fourth[:, body:].reshape(count, -1)[:, : 3 * mine * sum(widths)]
+    heard = heard.reshape(count, 3, mine, sum(widths)).astype(jnp.float32)
+    heard = (heard[:, 0] + heard[:, 1]) + heard[:, 2]
+    heard = heard.transpose(1, 0, 2)
+    query = heard[:, :, : widths[0]].reshape(mine, -1, HEAD_DIM)
+    key_new = heard[:, :, widths[0] : widths[0] + widths[1]].reshape(mine, -1, HEAD_DIM)
+    value_new = heard[:, :, widths[0] + widths[1] :].reshape(mine, -1, HEAD_DIM)
+    query = rotate(query, lengths).astype(jnp.bfloat16).reshape(mine, -1, group, HEAD_DIM)
+    key_new = rotate(key_new, lengths).astype(jnp.bfloat16)
+    attention_out = attend(
+        query, key_new, value_new.astype(jnp.bfloat16), key_cache, value_cache, lengths
+    )
     return (
         attention_out,
         query_rollout,

time: 918 us -> 734 us (0.80)
  Pallas kernels: 0 us -> 123 us
  waiting for transfers between devices: 581 us -> 474 us
  local copies, waits for them, and re-layouts: 160 us -> 61.6 us
  other arithmetic: 68.6 us -> 22.3 us
  blocking collectives: 37.7 us -> 4.19 us
  between operations: 16 us -> 1.61 us
    unnamed x2 -> x0, waiting for transfers between devices: 216 us -> none
    pallas_call x0 -> x10, Pallas kernels: none -> 123 us  [the longest x4 60.4 us: pack_columns(): pl.pallas_call(functools.partial(pack_columns_kernel, widths, rows, extra...]
    all_to_all x5, waiting for transfers between devices: 365 us -> 474 us  [exchange(): lax.all_to_all(after(blocks, *earlier), 'fsdp', split_axis=0, concat_axis...]
    convert_element_type x9 -> x1, local copies, waits for them, and re-layouts: 93.2 us -> 0.14 us  [per_device(): heard = heard.reshape(count, 3, mine, sum(widths)).astype(jnp.float32)]
    convert_element_type x6 -> x2, other arithmetic: 38.2 us -> 0.1 us  [the longest x1 0.09 us: split_float(): parts.append(part.astype(jnp.bfloat16))]
    pmax x1, blocking collectives: 37.7 us -> 4.19 us  [per_device(): peaks = lax.pmax(jnp.max(heard, axis=0), 'tp')]
    unnamed x28 -> x31, local copies, waits for them, and re-layouts: 47.2 us -> 50.7 us
  transfers between devices with their start and end apart: 6 -> 5, of which waited for: 5 -> 4; matrix products, arithmetic and copies ran while one was open for 25% -> 13% of each run, Pallas kernels for 0% -> 14%
where the time goes in v1:
time: 734 us; the launch traced here: 730 us
  waiting for transfers between devices  474 us (65%)
  Pallas kernels  123 us (17%)
  local copies, waits for them, and re-layouts  61.6 us (8%)
  starting transfers between devices  26.9 us (4%)
  other arithmetic  22.3 us (3%)
  matrix products  16.9 us (2%)
    all_to_all x5, waiting for transfers between devices, exchange(): lax.all_to_all(after(blocks, *earlier), 'fsdp', split_axis=0, concat_axis...  474 us
    pallas_call x4, Pallas kernels, pack_columns(): pl.pallas_call(functools.partial(pack_columns_kernel, widths, rows, extra...  60.4 us
    unnamed x31, local copies, waits for them, and re-layouts  50.7 us
    pallas_call x4, Pallas kernels, unpack_columns(): pl.pallas_call(functools.partial(unpack_columns_kernel, widths, numbers,...  43.7 us
    all_to_all x5, starting transfers between devices, exchange(): lax.all_to_all(after(blocks, *earlier), 'fsdp', split_axis=0, concat_axis...  26.9 us
    reduce_max x7, other arithmetic, largest(): return jnp.max(jnp.abs(tensor.astype(jnp.float32)))  19.9 us
  transfers between devices with their start and end apart: 5, of which 4 were waited for; matrix products, arithmetic and copies ran while one was open for 13% of the time, Pallas kernels for 14%

profile of v1, /device:TPU:13, one launch (start us, length us, event | category | flops | bytes accessed | tf_op | source)
XLA Modules:
  0.0 730.0 jit_solution(14352698929483903704)
XLA Ops:
  2.2 8.8 %shard_map.196 = bf16[16,480,128]{2,1,0:T(8,128)(2,1)} custom-call(bf16[160,5120]{1,0:T(8,128)(2,1)} %in_ref.1, bf16[1,80,128]{2,1,0:T(8,128)(2,1)} %reshape.478.extra_ref), custom_call_target="tpu_custom_call" | custom-call | flops 819200 | bytes 3276800 | tf_op jit(solution)/shard_map/pallas_call | solution.py:203
  11.0 6.5 all-to-all-start
  30.0 5.9 abs_reduce_fusion.2
  35.9 5.9 abs_reduce_fusion.1
  49.3 13.8 %shard_map.197 = bf16[16,576,128]{2,1,0:T(8,128)(2,1)} custom-call(bf16[5120,160]{1,0:T(8,128)(2,1)} %copy.102.refs_0_, bf16[5120,32]{1,0:T(8,128)(2,1)} %copy.103.refs_1_, bf16[5120,32]{1,0:T(8,128)(2,1)} %copy.104.refs_2_, bf16[1,16,128]{2,1,0:T(8,128)(2,1)} %bitcast.80), custom_call_target="tpu_custom_call" | custom-call | flops 1146880 | bytes 4587520 | tf_op jit(solution)/shard_map/pallas_call | solution.py:143
  64.3 6.0 all-to-all-start.1
  70.3 12.7 %copy.110.refs_0_ = bf16[5120,864]{1,0:T(8,128)(2,1)} copy(bf16[5120,864]{0,1:T(8,128)(2,1)} %param.18) | data formatting | bytes 17694720 | tf_op args[5]
  83.6 15.6 %shard_map.199 = bf16[16,2176,128]{2,1,0:T(8,128)(2,1)} custom-call(bf16[5120,864]{1,0:T(8,128)(2,1)} %copy.110.refs_0_, bf16[1,16,128]{2,1,0:T(8,128)(2,1)} %broadcast_in_dim.32.refs_1_), custom_call_target="tpu_custom_call" | custom-call | flops 4423680 | bytes 17694720 | tf_op jit(solution)/shard_map/pallas_call | solution.py:143
  99.2 24.2 %all-to-all-done.1.in_ref = bf16[16,576,128]{2,1,0:T(8,128)(2,1)S(1)} async-done(((bf16[16,576,128]{2,1,0:T(8,128)(2,1)}), bf16[16,576,128]{2,1,0:T(8,128)(2,1)S(1)}, u32[]{:S(2)}, u32[]{:S(2)}) %all-to-all-start.1) | async-done | bytes 2359328 | tf_op jit(solution)/shard_map/all_to_all | solution.py:54
  123.4 4.8 all-to-all-start.2
  128.2 12.7 %copy.109.refs_0_ = bf16[5120,864]{1,0:T(8,128)(2,1)} copy(bf16[5120,864]{0,1:T(8,128)(2,1)} %param.19) | data formatting | bytes 17694720 | tf_op args[6]
  155.8 15.5 %shard_map.198 = bf16[16,2176,128]{2,1,0:T(8,128)(2,1)} custom-call(bf16[5120,864]{1,0:T(8,128)(2,1)} %copy.109.refs_0_, bf16[16,16,128]{2,1,0:T(8,128)(2,1)} %bitcast.72), custom_call_target="tpu_custom_call" | custom-call | flops 4423680 | bytes 17694720 | tf_op jit(solution)/shard_map/pallas_call | solution.py:143
  171.3 150.4 %all-to-all-done.2.in_ref = bf16[16,2176,128]{2,1,0:T(8,128)(2,1)} async-done(((bf16[16,2176,128]{2,1,0:T(8,128)(2,1)}), bf16[16,2176,128]{2,1,0:T(8,128)(2,1)}, u32[]{:S(2)}, u32[]{:S(2)}) %all-to-all-start.2) | async-done | bytes 8912928 | tf_op jit(solution)/shard_map/all_to_all | solution.py:54
  326.5 12.7 %copy.120 = bf16[864,5120]{0,1:T(8,128)(2,1)} copy(bf16[864,5120]{1,0:T(8,128)(2,1)} %param.20) | data formatting | bytes 17694720 | tf_op args[7]
  339.2 15.5 %shard_map.204 = bf16[16,2176,128]{2,1,0:T(8,128)(2,1)} custom-call(bf16[5120,864]{1,0:T(8,128)(2,1)} %bitcast.67, bf16[1,16,128]{2,1,0:T(8,128)(2,1)} %broadcast_in_dim.32.refs_1_), custom_call_target="tpu_custom_call" | custom-call | flops 4423680 | bytes 17694720 | tf_op jit(solution)/shard_map/pallas_call | solution.py:143
  354.7 165.4 %all-to-all-done.3.in_ref = bf16[16,2176,128]{2,1,0:T(8,128)(2,1)} async-done(((bf16[16,2176,128]{2,1,0:T(8,128)(2,1)}), bf16[16,2176,128]{2,1,0:T(8,128)(2,1)}, u32[]{:S(2)}, u32[]{:S(2)}) %all-to-all-start.3) | async-done | bytes 8912928 | tf_op jit(solution)/shard_map/all_to_all | solution.py:54
  520.1 4.8 all-to-all-start.4
  525.2 9.8 %shard_map.201 = bf16[2560,320]{1,0:T(8,128)(2,1)} custom-call(f32[7]{0:T(128)} %copy-done.4, bf16[16,480,128]{2,1,0:T(8,128)(2,1)} %copy-done.1), custom_call_target="tpu_custom_call" | custom-call | flops 819200 | bytes 3276800 | tf_op jit(solution)/shard_map/pallas_call | solution.py:301
  538.9 8.9 %shard_map.200 = (bf16[320,2560]{1,0:T(8,128)(2,1)}, bf16[320,512]{1,0:T(8,128)(2,1)}, bf16[320,512]{1,0:T(8,128)(2,1)}) custom-call(f32[7]{0:T(128)} %copy-done.4, bf16[16,576,128]{2,1,0:T(8,128)(2,1)} %copy-done), custom_call_target="tpu_custom_call" | custom-call | flops 1146880 | bytes 4587520 | tf_op jit(solution)/shard_map/pallas_call | solution.py:272
  547.8 11.6 %shard_map.202 = bf16[320,13824]{1,0:T(8,128)(2,1)} custom-call(f32[7]{0:T(128)} %copy-done.4, bf16[16,2176,128]{2,1,0:T(8,128)(2,1)} %all-to-all-done.2.in_ref), custom_call_target="tpu_custom_call" | custom-call | flops 4423680 | bytes 17694720 | tf_op jit(solution)/shard_map/pallas_call | solution.py:272
  561.4 5.8 select_reduce_fusion
  573.0 11.6 %shard_map.203 = bf16[320,13824]{1,0:T(8,128)(2,1)} custom-call(f32[7]{0:T(128)} %copy-done.4, bf16[16,2176,128]{2,1,0:T(8,128)(2,1)} %all-to-all-done.3.in_ref), custom_call_target="tpu_custom_call" | custom-call | flops 4423680 | bytes 17694720 | tf_op jit(solution)/shard_map/pallas_call | solution.py:272
  584.5 133.9 %all-to-all-done.4.in_ref = bf16[16,2176,128]{2,1,0:T(8,128)(2,1)} async-done(((bf16[16,2176,128]{2,1,0:T(8,128)(2,1)}), bf16[16,2176,128]{2,1,0:T(8,128)(2,1)}, u32[]{:S(2)}, u32[]{:S(2)}) %all-to-all-start.4) | async-done | bytes 8912928 | tf_op jit(solution)/shard_map/all_to_all | solution.py:54
  718.5 11.6 %shard_map.205 = bf16[320,13824]{1,0:T(8,128)(2,1)} custom-call(f32[7]{0:T(128)} %copy-done.4, bf16[16,2176,128]{2,1,0:T(8,128)(2,1)} %all-to-all-done.4.in_ref), custom_call_target="tpu_custom_call" | custom-call | flops 4423680 | bytes 17694720 | tf_op jit(solution)/shard_map/pallas_call | solution.py:272
  (92 shorter events, 54.0 us)
Async XLA Ops:
  0.6 20.8 %copy-start.2 = (bf16[5120,32]{0,1:T(8,128)(2,1)S(1)}, bf16[5120,32]{0,1:T(8,128)(2,1)}, u32[]{:S(2)}) copy-start(bf16[5120,32]{0,1:T(8,128)(2,1)} %param.15) | copy-start | bytes 983044
  0.7 22.2 %copy-start.3 = (bf16[5120,32]{0,1:T(8,128)(2,1)S(1)}, bf16[5120,32]{0,1:T(8,128)(2,1)}, u32[]{:S(2)}) copy-start(bf16[5120,32]{0,1:T(8,128)(2,1)} %param.16) | copy-start | bytes 983044
  11.0 52.1 %all-to-all-start = ((bf16[16,480,128]{2,1,0:T(8,128)(2,1)}), bf16[16,480,128]{2,1,0:T(8,128)(2,1)S(1)}, u32[]{:S(2)}, u32[]{:S(2)}) async-start(bf16[16,480,128]{2,1,0:T(8,128)(2,1)} %shard_map.196), calls=%async_computation | async-start | bytes 3932160 | tf_op jit(solution)/shard_map/all_to_all | solution.py:54
  30.0 11.8 %slice-start = ((s8[8847360]{0:T(1024)(128)(4,1)}), s8[4194304]{0:T(1024)(128)(4,1)S(1)}, s32[]{:S(2)}) async-start(s8[8847360]{0:T(1024)(128)(4,1)} %bitcast.68), calls=%async_computation.5 | async-start | bytes 8388608
  30.0 11.8 %slice-start.1 = ((s8[8847360]{0:T(1024)(128)(4,1)}), s8[4194304]{0:T(1024)(128)(4,1)S(1)}, s32[]{:S(2)}) async-start(s8[8847360]{0:T(1024)(128)(4,1)} %bitcast.68), calls=%async_computation.6 | async-start | bytes 8388608
  35.9 5.9 slice-start.2
  63.0 1.3 copy-start.1
  64.3 59.1 %all-to-all-start.1 = ((bf16[16,576,128]{2,1,0:T(8,128)(2,1)}), bf16[16,576,128]{2,1,0:T(8,128)(2,1)S(1)}, u32[]{:S(2)}, u32[]{:S(2)}) async-start(bf16[16,576,128]{2,1,0:T(8,128)(2,1)} %shard_map.197), calls=%async_computation.1 | async-start | bytes 4718592 | tf_op jit(solution)/shard_map/all_to_all | solution.py:54
  123.4 19.0 %copy-start = (bf16[16,576,128]{2,1,0:T(8,128)(2,1)}, bf16[16,576,128]{2,1,0:T(8,128)(2,1)S(1)}, u32[]{:S(2)}) copy-start(bf16[16,576,128]{2,1,0:T(8,128)(2,1)S(1)} %all-to-all-done.1.in_ref) | copy-start | bytes 7077892
  123.4 198.4 %all-to-all-start.2 = ((bf16[16,2176,128]{2,1,0:T(8,128)(2,1)}), bf16[16,2176,128]{2,1,0:T(8,128)(2,1)}, u32[]{:S(2)}, u32[]{:S(2)}) async-start(bf16[16,2176,128]{2,1,0:T(8,128)(2,1)} %shard_map.199), calls=%async_computation.2 | async-start | bytes 17825792 | tf_op jit(solution)/shard_map/all_to_all | solution.py:54
  128.1 13.4 %slice-start.3 = ((bf16[16,480,128]{2,1,0:T(8,128)(2,1)}), bf16[16,80,128]{2,1,0:T(8,128)(2,1)S(1)}, s32[]{:S(2)}) async-start(bf16[16,480,128]{2,1,0:T(8,128)(2,1)} %copy-done.1), calls=%async_computation.8 | async-start | bytes 655360 | tf_op jit(solution)/shard_map/slice | solution.py:405
  128.2 18.8 %copy-start.5 = (f32[7,1024]{1,0:T(8,128)S(1)}, f32[7,1024]{1,0:T(8,128)}, u32[]{:S(2)}) copy-start(f32[7,1024]{1,0:T(8,128)} %param.21) | copy-start | bytes 86020
  147.8 23.6 %copy-start.4 = (f32[7]{0:T(128)}, f32[7]{0:T(128)S(1)}, u32[]{:S(2)}) copy-start(f32[7]{0:T(128)S(1)} %maximum_divide_fusion.factor_ref) | copy-start | bytes 88
  321.7 198.4 %all-to-all-start.3 = ((bf16[16,2176,128]{2,1,0:T(8,128)(2,1)}), bf16[16,2176,128]{2,1,0:T(8,128)(2,1)}, u32[]{:S(2)}, u32[]{:S(2)}) async-start(bf16[16,2176,128]{2,1,0:T(8,128)(2,1)} %shard_map.198), calls=%async_computation.3 | async-start | bytes 17825792 | tf_op jit(solution)/shard_map/all_to_all | solution.py:54
  354.7 170.2 %copy-start.6 = (s32[2]{0:T(128)S(1)}, s32[2]{0:T(128)}, u32[]{:S(2)}) copy-start(s32[2]{0:T(128)} %param.23) | copy-start | bytes 28
  520.1 198.4 %all-to-all-start.4 = ((bf16[16,2176,128]{2,1,0:T(8,128)(2,1)}), bf16[16,2176,128]{2,1,0:T(8,128)(2,1)}, u32[]{:S(2)}, u32[]{:S(2)}) async-start(bf16[16,2176,128]{2,1,0:T(8,128)(2,1)} %shard_map.204), calls=%async_computation.4 | async-start | bytes 17825792 | tf_op jit(solution)/shard_map/all_to_all | solution.py:54

commit v2 on v1

--- a/solution.py
+++ b/solution.py
@@ -7,6 +7,7 @@
 from jax.experimental import pallas as pl
 from jax.experimental.pallas import tpu as pltpu
 from jax.sharding import PartitionSpec as P
+
 
 HEAD_DIM = 128
 LANES = 128
@@ -85,6 +86,10 @@
     return tiles
 
 
+def slab_of(rows, limit):
+    return max(slab for slab in range(SLAB, limit + 1, SLAB) if rows % slab == 0)
+
+
 def cost(count):
     return pl.CostEstimate(flops=count, bytes_accessed=4 * count, transcendentals=0)
 
@@ -99,7 +104,7 @@
 
 
 def pack_columns_kernel(widths, rows, extra, *refs):
-    ins, extra_ref, out_ref, rest_ref = refs[: len(widths)], refs[-3], refs[-2], refs[-1]
+    ins, out_ref, rest_ref = refs[: len(widths)], refs[-2], refs[-1]
     total = sum(widths)
     fold = folds(total)
     full, rest = total // LANES, total % LANES
@@ -109,6 +114,7 @@
         out_ref[0, pl.ds(tile * rows, rows), :] = ins[0][:, tile * LANES : (tile + 1) * LANES]
     if rest:
         group = rows // fold
+        slab = slab_of(group, 80)
         splits = [lead - full * LANES] + list(widths[1:])
         for number, size in enumerate(splits):
             first = full * LANES if number == 0 else 0
@@ -117,47 +123,50 @@
         def step(index, carry):
             pieces = []
             for part in range(fold):
-                low = pl.multiple_of(part * group + index * SLAB, SLAB)
+                low = pl.multiple_of(part * group + index * slab, SLAB)
                 for number, size in enumerate(splits):
-                    pieces.append((rest_ref[number, pl.ds(low, SLAB), :], 0, size))
+                    pieces.append((rest_ref[number, pl.ds(low, slab), :], 0, size))
             for tile, value in enumerate(assemble(pieces)):
-                low = pl.multiple_of(full * rows + tile * group + index * SLAB, SLAB)
-                out_ref[0, pl.ds(low, SLAB), :] = value.astype(jnp.bfloat16)
+                low = pl.multiple_of(full * rows + tile * group + index * slab, SLAB)
+                out_ref[0, pl.ds(low, slab), :] = value.astype(jnp.bfloat16)
             return carry
 
-        lax.fori_loop(0, group // SLAB, step, 0)
+        lax.fori_loop(0, group // slab, step, 0)
     if extra:
-        out_ref[0, pl.ds(tile_rows(rows, total), extra), :] = extra_ref[0]
-
-
-def pack_columns(count, tensors, extra):
+        out_ref[0, pl.ds(tile_rows(rows, total), extra), :] = refs[len(widths)][0]
+
+
+def with_extra(count, flat, extra):
+    if extra is None:
+        return flat
+    return jnp.concatenate([flat, jnp.broadcast_to(extra, (count,) + extra.shape[1:])], axis=1)
+
+
+def pack_columns(count, tensors, extra=None):
     rows = tensors[0].shape[0] // count
     widths = [tensor.shape[1] for tensor in tensors]
     body = tile_rows(rows, sum(widths))
     if not columns_fit(count, rows, sum(widths)):
         joined = jnp.concatenate(tensors, axis=1) if len(tensors) > 1 else tensors[0]
         flat = joined.reshape(count, -1, LANES)
-        return jnp.concatenate([flat, jnp.broadcast_to(extra, (count,) + extra.shape[1:])], axis=1)
-    extra_rows = extra.shape[1]
-    shared = extra.shape[0] == 1
+        return with_extra(count, flat, extra)
+    extras = [] if extra is None else [extra]
+    extra_rows = 0 if extra is None else extra.shape[1]
     return pl.pallas_call(
         functools.partial(pack_columns_kernel, widths, rows, extra_rows),
         grid=(count,),
         in_specs=[pl.BlockSpec((rows, width), lambda f: (f, 0)) for width in widths]
-        + [
-            pl.BlockSpec(
-                (1, extra_rows, LANES), (lambda f: (0, 0, 0)) if shared else (lambda f: (f, 0, 0))
-            )
-        ],
+        + [pl.BlockSpec((1, extra_rows, LANES), lambda f: (0, 0, 0)) for _ in extras],
         out_specs=pl.BlockSpec((1, body + extra_rows, LANES), lambda f: (f, 0, 0)),
         out_shape=jax.ShapeDtypeStruct((count, body + extra_rows, LANES), jnp.bfloat16),
         scratch_shapes=[pltpu.VMEM((len(widths), rows, LANES), jnp.float32)],
         cost_estimate=cost(count * body * LANES),
-    )(*tensors, extra)
+    )(*tensors, *extras)
 
 
 def pack_rows_kernel(rows, width, extra, in_ref, extra_ref, out_ref):
     full, half = width // LANES, rows // 2
+    slab = slab_of(half, 80)
     for side in range(2):
         if side == 0:
             for tile in range(full):
@@ -168,9 +177,9 @@
         def step(index, carry):
             lasts = []
             for part in range(2):
-                low = pl.multiple_of(part * half + index * SLAB, SLAB)
+                low = pl.multiple_of(part * half + index * slab, SLAB)
                 values = [
-                    in_ref[pl.ds(low, SLAB), tile * LANES : (tile + 1) * LANES].astype(jnp.float32)
+                    in_ref[pl.ds(low, slab), tile * LANES : (tile + 1) * LANES].astype(jnp.float32)
                     for tile in range(side * full, side * full + full + 1)
                 ]
                 if side == 0:
@@ -180,14 +189,14 @@
                     pieces += [(value, 0, LANES) for value in values[1:-1]]
                     pieces += [(values[-1], 0, LANES // 2)]
                     for tile, value in enumerate(assemble(pieces)):
-                        to = pl.multiple_of(tile * rows + part * half + index * SLAB, SLAB)
-                        out_ref[1, pl.ds(to, SLAB), :] = value.astype(jnp.bfloat16)
+                        to = pl.multiple_of(tile * rows + part * half + index * slab, SLAB)
+                        out_ref[1, pl.ds(to, slab), :] = value.astype(jnp.bfloat16)
                     lasts.append((values[-1], LANES // 2, LANES // 2))
-            to = pl.multiple_of(full * rows + index * SLAB, SLAB)
-            out_ref[side, pl.ds(to, SLAB), :] = assemble(lasts)[0].astype(jnp.bfloat16)
+            to = pl.multiple_of(full * rows + index * slab, SLAB)
+            out_ref[side, pl.ds(to, slab), :] = assemble(lasts)[0].astype(jnp.bfloat16)
             return carry
 
-        lax.fori_loop(0, half // SLAB, step, 0)
+        lax.fori_loop(0, half // slab, step, 0)
         if extra:
             out_ref[side, pl.ds(tile_rows(rows, width), extra), :] = extra_ref[0]
 
@@ -199,7 +208,7 @@
     extra_rows = extra.shape[1]
     if not rows_fit(count, rows, width):
         flat = tensor.reshape(rows, count, width).transpose(1, 0, 2).reshape(count, -1, LANES)
-        return jnp.concatenate([flat, jnp.broadcast_to(extra, (count,) + extra.shape[1:])], axis=1)
+        return with_extra(count, flat, extra)
     return pl.pallas_call(
         functools.partial(pack_rows_kernel, rows, width, extra_rows),
         grid=(count // 2,),
@@ -223,17 +232,17 @@
 
         def step(index, carry):
             pieces = [[] for _ in widths]
-            low = pl.multiple_of(part * group + index * SLAB, SLAB)
+            low = part * group + index * SLAB
             for source in range(sources):
                 have = []
                 for tile in range(full):
-                    at = pl.multiple_of(tile * rows + part * group + index * SLAB, SLAB)
+                    at = tile * rows + part * group + index * SLAB
                     have.append((in_ref[source, pl.ds(at, SLAB), :].astype(jnp.float32), 0, LANES))
                 first = part * rest
                 while first < (part + 1) * rest:
                     tile = first // LANES
                     last = min((part + 1) * rest, (tile + 1) * LANES)
-                    at = pl.multiple_of(full * rows + tile * group + index * SLAB, SLAB)
+                    at = full * rows + tile * group + index * SLAB
                     value = in_ref[source, pl.ds(at, SLAB), :].astype(jnp.float32)
                     have.append((value, first - tile * LANES, last - first))
                     first = last
@@ -254,7 +263,8 @@
                     ).astype(jnp.bfloat16)
             return carry
 
-        lax.fori_loop(0, group // SLAB, step, 0)
+        for index in range(group // SLAB):
+            step(index, 0)
 
 
 def unpack_columns(count, arrived, rows, widths, factors, numbers):
@@ -318,13 +328,61 @@
     return jnp.pad(values, ((0, 0), (0, room - size))).reshape(lead, room // LANES, LANES)
 
 
-def split_float(values):
-    parts = []
-    for _ in range(3):
-        part = lax.reduce_precision(values, 8, 7)
-        parts.append(part.astype(jnp.bfloat16))
-        values = values - part
-    return jnp.stack(parts)
+def shifted(block_for, steps):
+    count = lax.axis_size("fsdp")
+    here = lax.axis_index("fsdp")
+    return {
+        step: lax.ppermute(
+            block_for((here + step) % count),
+            "fsdp",
+            [(place, (place + step) % count) for place in range(count)],
+        )
+        for step in steps
+    }
+
+
+def by_source(own, received):
+    count = lax.axis_size("fsdp")
+    blocks = jnp.stack([received[step] for step in range(count - 1, 0, -1)] + [own])
+    twice = jnp.concatenate([blocks, blocks])
+    return lax.dynamic_slice_in_dim(twice, count - 1 - lax.axis_index("fsdp"), count)
+
+
+def maxima_kernel(*refs):
+    ins, out_ref, seen_ref = refs[:-2], refs[-2], refs[-1]
+    step = pl.program_id(0)
+    for number, in_ref in enumerate(ins):
+        sizes = jnp.abs(in_ref[...])
+        rows, width = sizes.shape
+        most = jnp.max(sizes.reshape(rows // SLAB, SLAB, width), axis=0).astype(jnp.float32)
+        tiles = [most[:, low : low + LANES] for low in range(0, width, LANES)]
+        best = functools.reduce(jnp.maximum, tiles)
+        seen_ref[number] = jnp.where(step == 0, best, jnp.maximum(seen_ref[number], best))
+
+    @pl.when(step == pl.num_programs(0) - 1)
+    def _():
+        lanes = lane_index(SLAB)
+        total = jnp.zeros((SLAB, LANES), jnp.float32)
+        for number in range(len(ins)):
+            total = jnp.where(lanes == number, jnp.max(seen_ref[number]), total)
+        out_ref[0] = total.astype(jnp.bfloat16)
+
+
+def maxima(tensors):
+    blocks = 8
+    width = tensors[0].shape[1] // blocks
+    if width % LANES or any(tensor.shape[0] % SLAB for tensor in tensors):
+        local = jnp.stack([largest(tensor) for tensor in tensors])
+        return padded_rows(local[None, :].astype(jnp.bfloat16), SLAB)
+    return pl.pallas_call(
+        maxima_kernel,
+        grid=(blocks,),
+        in_specs=[pl.BlockSpec((tensor.shape[0], width), lambda f: (0, f)) for tensor in tensors],
+        out_specs=pl.BlockSpec((1, SLAB, LANES), lambda f: (0, 0, 0)),
+        out_shape=jax.ShapeDtypeStruct((1, SLAB, LANES), jnp.bfloat16),
+        scratch_shapes=[pltpu.VMEM((len(tensors), SLAB, LANES), jnp.float32)],
+        cost_estimate=cost(sum(tensor.size for tensor in tensors) // 2),
+    )(*tensors)
 
 
 def attend(query, key_new, value_new, key_cache, value_cache, lengths):
@@ -391,13 +449,27 @@
 
     sent_hidden = hidden.reshape(1, -1, LANES)
     first = exchange(pack_rows(count, output_weight, sent_hidden))
-    local = jnp.stack([largest(tensor) for tensor in trainer])
-    sent_local = padded_rows(local[None, :].astype(jnp.bfloat16), SLAB)
-    second = exchange(pack_columns(count, trainer[:3], sent_local), first)
-    none = jnp.zeros((1, SLAB, LANES), jnp.bfloat16)
-    third = exchange(pack_columns(count, (gate_weight,), none), second)
-
-    body = tile_rows(rows, sum(widths))
+    packed = pack_columns(count, trainer[:3])
+
+    def block_of(blocks):
+        return lambda device: lax.dynamic_index_in_dim(blocks, device, 0, keepdims=False)
+
+    received = {}
+    steps = range(1, count)
+    bridges = [count // 2, count // 2 - 1, count // 2 + 1, count // 2 - 2]
+    received |= shifted(block_of(packed), [step for step in steps if step not in bridges])
+    flat = [tensor.T for tensor in trainer]
+    flat[3], flat[6] = output_weight, down_weight
+    sent = pack_rows(count, down_weight, maxima(flat))
+    second = exchange(sent, first)
+    ready = after(packed, first)
+    received |= shifted(block_of(ready), bridges[:2])
+    sent = pack_columns(count, (after(up_weight, first),))
+    third = exchange(sent, second)
+    ready = after(packed, second)
+    received |= shifted(block_of(ready), bridges[2:])
+
+    body = tile_rows(down_weight.shape[0], rows)
     heard = second[:, body:].reshape(count, -1)[:, :7].astype(jnp.float32)
     peaks = lax.pmax(jnp.max(heard, axis=0), "tp")
     factors, new_history = scaling(peaks, history, slot)
@@ -419,24 +491,13 @@
         ],
         axis=1,
     )
-    pieces = split_float(fresh).reshape(3, count, mine, -1).transpose(1, 0, 2, 3)
-    sent_fresh = padded_rows(pieces.reshape(count, -1), SLAB)
-    fourth = exchange(pack_columns(count, (up_weight,), sent_fresh), third)
-    fifth = exchange(pack_columns(count, (down_weight.T,), none), fourth)
-
-    query_rollout, key_rollout, value_rollout = unpack_columns(
-        count, second, rows, widths, factors, (0, 1, 2)
-    )
-    output_rollout = unpack_rows(count, first, output_weight.shape[0], rows, factors, 3)
-    (gate_rollout,) = unpack_columns(count, third, rows, [gate_weight.shape[1]], factors, (4,))
-    (up_rollout,) = unpack_columns(count, fourth, rows, [up_weight.shape[1]], factors, (5,))
-    (down_rollout,) = unpack_columns(count, fifth, rows, [down_weight.shape[0]], factors, (6,))
-    down_rollout = down_rollout.T
-
-    body = tile_rows(rows, up_weight.shape[1])
-    heard = fourth[:, body:].reshape(count, -1)[:, : 3 * mine * sum(widths)]
-    heard = heard.reshape(count, 3, mine, sum(widths)).astype(jnp.float32)
-    heard = (heard[:, 0] + heard[:, 1]) + heard[:, 2]
+    fresh = fresh.reshape(count, mine, -1)
+    heard = by_source(
+        block_of(fresh)(lax.axis_index("fsdp")), shifted(block_of(fresh), steps)
+    )
+    sent = pack_columns(count, (after(gate_weight, second),))
+    fourth = exchange(sent, third)
+
     heard = heard.transpose(1, 0, 2)
     query = heard[:, :, : widths[0]].reshape(mine, -1, HEAD_DIM)
     key_new = heard[:, :, widths[0] : widths[0] + widths[1]].reshape(mine, -1, HEAD_DIM)
@@ -445,6 +506,15 @@
     key_new = rotate(key_new, lengths).astype(jnp.bfloat16)
     attention_out = attend(
         query, key_new, value_new.astype(jnp.bfloat16), key_cache, value_cache, lengths
+    )
+    output_rollout = unpack_rows(count, first, output_weight.shape[0], rows, factors, 3)
+    down_rollout = unpack_rows(count, second, down_weight.shape[0], rows, factors, 6)
+    (gate_rollout,) = unpack_columns(count, fourth, rows, [gate_weight.shape[1]], factors, (4,))
+    (up_rollout,) = unpack_columns(count, third, rows, [up_weight.shape[1]], factors, (5,))
+    received = lax.optimization_barrier((received, attention_out))[0]
+    arrived = by_source(block_of(packed)(lax.axis_index("fsdp")), received)
+    query_rollout, key_rollout, value_rollout = unpack_columns(
+        count, arrived, rows, widths, factors, (0, 1, 2)
     )
     return (
         attention_out,

time: 734 us -> 797 us (1.086)
  starting transfers between devices: 26.9 us -> 81.4 us
  waiting for transfers between devices: 474 us -> 505 us
  other arithmetic: 22.3 us -> 3.14 us
  Pallas kernels: 123 us -> 115 us
    ppermute x0 -> x30, waiting for transfers between devices: none -> 154 us  [shifted(): lax.ppermute(block_for((here + step) % count), 'fsdp', [(place, (place +...]
    all_to_all x5 -> x4, waiting for transfers between devices: 474 us -> 352 us  [exchange(): lax.all_to_all(after(blocks, *earlier), 'fsdp', split_axis=0, concat_axis...]
    ppermute x0 -> x30, starting transfers between devices: none -> 60.5 us  [shifted(): lax.ppermute(block_for((here + step) % count), 'fsdp', [(place, (place +...]
    unnamed x31 -> x62, local copies, waits for them, and re-layouts: 50.7 us -> 25.3 us
    optimization_barrier x0 -> x2, local copies, waits for them, and re-layouts: none -> 25.4 us  [after(): return lax.optimization_barrier((tensor,) + earlier)[0]]
    pallas_call x4 -> x3, Pallas kernels: 60.4 us -> 36.5 us  [pack_columns(): pl.pallas_call(functools.partial(pack_columns_kernel, widths, rows, extra...]
    pallas_call x4 -> x3, Pallas kernels: 43.7 us -> 21.6 us  [unpack_columns(): pl.pallas_call(functools.partial(unpack_columns_kernel, widths, numbers,...]
    reduce_max x7 -> x0, other arithmetic: 19.9 us -> none  [largest(): return jnp.max(jnp.abs(tensor.astype(jnp.float32)))]
  transfers between devices with their start and end apart: 5 -> 34, of which waited for: 4 -> 5; matrix products, arithmetic and copies ran while one was open for 13% -> 10% of each run, Pallas kernels for 14% -> 13%
where the time goes in v2:
time: 797 us; the launch traced here: 789 us
  waiting for transfers between devices  505 us (63%)
  Pallas kernels  115 us (14%)
  starting transfers between devices  81.4 us (10%)
  local copies, waits for them, and re-layouts  62.6 us (8%)
  matrix products  15.1 us (2%)
    all_to_all x4, waiting for transfers between devices, exchange(): lax.all_to_all(after(blocks, *earlier), 'fsdp', split_axis=0, concat_axis...  352 us
    ppermute x30, waiting for transfers between devices, shifted(): lax.ppermute(block_for((here + step) % count), 'fsdp', [(place, (place +...  154 us
    ppermute x30, starting transfers between devices, shifted(): lax.ppermute(block_for((here + step) % count), 'fsdp', [(place, (place +...  60.5 us
    pallas_call x3, Pallas kernels, pack_columns(): pl.pallas_call(functools.partial(pack_columns_kernel, widths, rows, extra...  36.5 us
    optimization_barrier x2, local copies, waits for them, and re-layouts, after(): return lax.optimization_barrier((tensor,) + earlier)[0]  25.4 us
    unnamed x62, local copies, waits for them, and re-layouts  25.3 us
    pallas_call x2, Pallas kernels, unpack_rows(): pl.pallas_call(functools.partial(unpack_rows_kernel, number, rows, width)...  23.4 us
    pallas_call x3, Pallas kernels, unpack_columns(): pl.pallas_call(functools.partial(unpack_columns_kernel, widths, numbers,...  21.6 us
  transfers between devices with their start and end apart: 34, of which 5 were waited for; matrix products, arithmetic and copies ran while one was open for 10% of the time, Pallas kernels for 13%

profile of v2, /device:TPU:13, one launch (start us, length us, event | category | flops | bytes accessed | tf_op | source)
XLA Modules:
  0.0 789.0 jit_solution(10622510565445276678)
XLA Ops:
  2.1 5.9 shard_map.196
  8.0 6.5 all-to-all-start
  14.5 12.3 %shard_map.197.extra_ref = bf16[1,16,128]{2,1,0:T(8,128)(2,1)} custom-call(bf16[160,5120]{1,0:T(8,128)(2,1)} %bitcast.156, bf16[32,5120]{1,0:T(8,128)(2,1)} %bitcast.159, bf16[32,5120]{1,0:T(8,128)(2,1)} %bitcast.158, bf16[160,5120]{1,0:T(8,128)(2,1)} %refs_3_.1, bf16[864,5120]{1,0:T(8,128)(2,1)} %bitcast.155, bf16[864,5120]{1,0:T(8,128)(2,1)} %bitcast.154, ...), custom_call_target="tpu_custom_call" | custom-call | flops 7618560 | bytes 30474240 | tf_op jit(solution)/shard_map/pallas_call | solution.py:377
  26.8 15.3 %shard_map.198 = bf16[16,2176,128]{2,1,0:T(8,128)(2,1)} custom-call(bf16[864,5120]{1,0:T(8,128)(2,1)} %in_ref.3, bf16[1,16,128]{2,1,0:T(8,128)(2,1)} %shard_map.197.extra_ref), custom_call_target="tpu_custom_call" | custom-call | flops 4423680 | bytes 17694720 | tf_op jit(solution)/shard_map/pallas_call | solution.py:212
  42.1 17.0 %all-to-all-done.in_ref = bf16[16,480,128]{2,1,0:T(8,128)(2,1)S(1)} async-done(((bf16[16,480,128]{2,1,0:T(8,128)(2,1)}), bf16[16,480,128]{2,1,0:T(8,128)(2,1)S(1)}, u32[]{:S(2)}, u32[]{:S(2)}) %all-to-all-start) | async-done | bytes 1966112 | tf_op jit(solution)/shard_map/all_to_all | solution.py:55
  59.1 4.8 all-to-all-start.1
  63.9 12.7 %copy.43.refs_0_ = bf16[5120,864]{1,0:T(8,128)(2,1)} copy(bf16[5120,864]{0,1:T(8,128)(2,1)} %param.19) | data formatting | bytes 17694720 | tf_op jit(solution)/shard_map/optimization_barrier | solution.py:51
  76.6 12.7 %shard_map.203 = bf16[16,2160,128]{2,1,0:T(8,128)(2,1)} custom-call(bf16[5120,864]{1,0:T(8,128)(2,1)} %copy.43.refs_0_), custom_call_target="tpu_custom_call" | custom-call | flops 4423680 | bytes 17694720 | tf_op jit(solution)/shard_map/pallas_call | solution.py:155
  89.3 168.2 %all-to-all-done.1.in_ref = bf16[16,2176,128]{2,1,0:T(8,128)(2,1)} async-done(((bf16[16,2176,128]{2,1,0:T(8,128)(2,1)}), bf16[16,2176,128]{2,1,0:T(8,128)(2,1)}, u32[]{:S(2)}, u32[]{:S(2)}) %all-to-all-start.1) | async-done | bytes 8912928 | tf_op jit(solution)/shard_map/all_to_all | solution.py:55
  257.5 4.8 all-to-all-start.2
  262.2 12.7 %copy.42.refs_0_ = bf16[5120,864]{1,0:T(8,128)(2,1)} copy(bf16[5120,864]{0,1:T(8,128)(2,1)} %param.18) | data formatting | bytes 17694720 | tf_op jit(solution)/shard_map/optimization_barrier | solution.py:51
  274.9 12.7 %shard_map.202 = bf16[16,2160,128]{2,1,0:T(8,128)(2,1)} custom-call(bf16[5120,864]{1,0:T(8,128)(2,1)} %copy.42.refs_0_), custom_call_target="tpu_custom_call" | custom-call | flops 4423680 | bytes 17694720 | tf_op jit(solution)/shard_map/pallas_call | solution.py:155
  287.6 166.8 %all-to-all-done.2.in_ref = bf16[16,2160,128]{2,1,0:T(8,128)(2,1)} async-done(((bf16[16,2160,128]{2,1,0:T(8,128)(2,1)}), bf16[16,2160,128]{2,1,0:T(8,128)(2,1)}, u32[]{:S(2)}, u32[]{:S(2)}) %all-to-all-start.2) | async-done | bytes 8847392 | tf_op jit(solution)/shard_map/all_to_all | solution.py:55
  466.9 11.1 %shard_map.199 = bf16[16,560,128]{2,1,0:T(8,128)(2,1)} custom-call(bf16[5120,160]{1,0:T(8,128)(2,1)} %copy.39.refs_0_, bf16[5120,32]{1,0:T(8,128)(2,1)} %copy.40.refs_1_, bf16[5120,32]{1,0:T(8,128)(2,1)} %copy.41.refs_2_), custom_call_target="tpu_custom_call" | custom-call | flops 1146880 | bytes 4587520 | tf_op jit(solution)/shard_map/pallas_call | solution.py:155
  502.3 146.9 %collective-permute-done.14 = f32[2,224]{1,0:T(2,128)S(1)} collective-permute-done((f32[2,224]{1,0:T(2,128)S(1)}, f32[2,224]{1,0:T(2,128)S(1)}, u32[]{:S(2)}, u32[]{:S(2)}) %collective-permute-start.14) | collective-permute-done | bytes 1824 | tf_op jit(solution)/shard_map/ppermute | solution.py:335
  659.7 9.8 %shard_map.201 = bf16[2560,320]{1,0:T(8,128)(2,1)} custom-call(f32[7]{0:T(128)} %copy-done.10, bf16[16,480,128]{2,1,0:T(8,128)(2,1)} %copy-done), custom_call_target="tpu_custom_call" | custom-call | flops 819200 | bytes 3276800 | tf_op jit(solution)/shard_map/pallas_call | solution.py:311
  677.4 13.6 %shard_map.206 = bf16[13824,320]{1,0:T(8,128)(2,1)} custom-call(f32[7]{0:T(128)} %copy-done.10, bf16[16,2176,128]{2,1,0:T(8,128)(2,1)} %all-to-all-done.1.in_ref), custom_call_target="tpu_custom_call" | custom-call | flops 4423680 | bytes 17694720 | tf_op jit(solution)/shard_map/pallas_call | solution.py:311
  690.9 13.1 %copy.45 = bf16[13824,320]{0,1:T(8,128)(2,1)} copy(bf16[13824,320]{1,0:T(8,128)(2,1)} %shard_map.206) | data formatting | bytes 17694720
  711.5 5.8 select_reduce_fusion
  722.4 11.0 %collective-permute-start.16 = (bf16[560,128]{1,0:T(8,128)(2,1)S(1)}, bf16[560,128]{1,0:T(8,128)(2,1)S(1)}, u32[]{:S(2)}, u32[]{:S(2)}) collective-permute-start(bf16[560,128]{1,0:T(8,128)(2,1)S(1)} %get-tuple-element.86), channel_id=1, source_target_pairs={{0,4},{2,6},{4,8},{6,10},{8,12},{10,14},{12,16},{14,18},{16,20},{1... | collective-permute-start | bytes 430088 | tf_op jit(solution)/shard_map/ppermute | solution.py:335
  737.4 13.7 %collective-permute-start.23 = (bf16[560,128]{1,0:T(8,128)(2,1)S(1)}, bf16[560,128]{1,0:T(8,128)(2,1)S(1)}, u32[]{:S(2)}, u32[]{:S(2)}) collective-permute-start(bf16[560,128]{1,0:T(8,128)(2,1)S(1)} %get-tuple-element.88), channel_id=1, source_target_pairs={{0,18},{2,20},{4,22},{6,24},{8,26},{10,28},{12,30},{14,0},{16,2},{... | collective-permute-start | bytes 430088 | tf_op jit(solution)/shard_map/ppermute | solution.py:335
  756.5 6.6 collective-permute-done.20
  771.9 8.6 %shard_map.205 = bf16[320,13824]{1,0:T(8,128)(2,1)} custom-call(f32[7]{0:T(128)} %copy-done.10, bf16[16,2160,128]{2,1,0:T(8,128)(2,1)} %all-to-all-done.2.in_ref), custom_call_target="tpu_custom_call" | custom-call | flops 4423680 | bytes 17694720 | tf_op jit(solution)/shard_map/pallas_call | solution.py:282
  780.4 8.6 %shard_map.204 = bf16[320,13824]{1,0:T(8,128)(2,1)} custom-call(f32[7]{0:T(128)} %copy-done.10, bf16[16,2160,128]{2,1,0:T(8,128)(2,1)} %all-to-all-done.3.in_ref), custom_call_target="tpu_custom_call" | custom-call | flops 4423680 | bytes 17694720 | tf_op jit(solution)/shard_map/pallas_call | solution.py:282
  (184 shorter events, 85.8 us)
Async XLA Ops:
  8.0 51.1 %all-to-all-start = ((bf16[16,480,128]{2,1,0:T(8,128)(2,1)}), bf16[16,480,128]{2,1,0:T(8,128)(2,1)S(1)}, u32[]{:S(2)}, u32[]{:S(2)}) async-start(bf16[16,480,128]{2,1,0:T(8,128)(2,1)} %shard_map.196), calls=%async_computation | async-start | bytes 3932160 | tf_op jit(solution)/shard_map/all_to_all | solution.py:55
  59.1 198.4 %all-to-all-start.1 = ((bf16[16,2176,128]{2,1,0:T(8,128)(2,1)}), bf16[16,2176,128]{2,1,0:T(8,128)(2,1)}, u32[]{:S(2)}, u32[]{:S(2)}) async-start(bf16[16,2176,128]{2,1,0:T(8,128)(2,1)} %shard_map.198), calls=%async_computation.1 | async-start | bytes 17825792 | tf_op jit(solution)/shard_map/all_to_all | solution.py:55
  257.5 197.0 %all-to-all-start.2 = ((bf16[16,2160,128]{2,1,0:T(8,128)(2,1)}), bf16[16,2160,128]{2,1,0:T(8,128)(2,1)}, u32[]{:S(2)}, u32[]{:S(2)}) async-start(bf16[16,2160,128]{2,1,0:T(8,128)(2,1)} %shard_map.203), calls=%async_computation.2 | async-start | bytes 17694720 | tf_op jit(solution)/shard_map/all_to_all | solution.py:55
  454.4 326.0 %all-to-all-start.3 = ((bf16[16,2160,128]{2,1,0:T(8,128)(2,1)}), bf16[16,2160,128]{2,1,0:T(8,128)(2,1)}, u32[]{:S(2)}, u32[]{:S(2)}) async-start(bf16[16,2160,128]{2,1,0:T(8,128)(2,1)} %shard_map.202), calls=%async_computation.3 | async-start | bytes 17694720 | tf_op jit(solution)/shard_map/all_to_all | solution.py:55
  493.7 155.4 %collective-permute-start.14 = (f32[2,224]{1,0:T(2,128)S(1)}, f32[2,224]{1,0:T(2,128)S(1)}, u32[]{:S(2)}, u32[]{:S(2)}) collective-permute-start(f32[2,224]{1,0:T(2,128)S(1)} %get-tuple-element.95), channel_id=1, source_target_pairs={{0,2},{2,4},{4,6},{6,8},{8,10},{10,12},{12,14},{14,16},{16,18},{18... | collective-permute-start | bytes 5384 | tf_op jit(solution)/shard_map/ppermute | solution.py:335
  496.1 153.0 %collective-permute-start.13 = (f32[2,224]{1,0:T(2,128)S(1)}, f32[2,224]{1,0:T(2,128)S(1)}, u32[]{:S(2)}, u32[]{:S(2)}) collective-permute-start(f32[2,224]{1,0:T(2,128)S(1)} %get-tuple-element.96), channel_id=1, source_target_pairs={{0,4},{2,6},{4,8},{6,10},{8,12},{10,14},{12,16},{14,18},{16,20},{1... | collective-permute-start | bytes 5384 | tf_op jit(solution)/shard_map/ppermute | solution.py:335
  497.2 152.0 %collective-permute-start.12 = (f32[2,224]{1,0:T(2,128)S(1)}, f32[2,224]{1,0:T(2,128)S(1)}, u32[]{:S(2)}, u32[]{:S(2)}) collective-permute-start(f32[2,224]{1,0:T(2,128)S(1)} %get-tuple-element.97), channel_id=1, source_target_pairs={{0,6},{2,8},{4,10},{6,12},{8,14},{10,16},{12,18},{14,20},{16,22},{... | collective-permute-start | bytes 5384 | tf_op jit(solution)/shard_map/ppermute | solution.py:335
  497.5 155.0 %collective-permute-start.11 = (f32[2,224]{1,0:T(2,128)S(1)}, f32[2,224]{1,0:T(2,128)S(1)}, u32[]{:S(2)}, u32[]{:S(2)}) collective-permute-start(f32[2,224]{1,0:T(2,128)S(1)} %get-tuple-element.98), channel_id=1, source_target_pairs={{0,8},{2,10},{4,12},{6,14},{8,16},{10,18},{12,20},{14,22},{16,24},... | collective-permute-start | bytes 5384 | tf_op jit(solution)/shard_map/ppermute | solution.py:335
  498.4 156.4 %collective-permute-start.10 = (f32[2,224]{1,0:T(2,128)S(1)}, f32[2,224]{1,0:T(2,128)S(1)}, u32[]{:S(2)}, u32[]{:S(2)}) collective-permute-start(f32[2,224]{1,0:T(2,128)S(1)} %get-tuple-element.99), channel_id=1, source_target_pairs={{0,10},{2,12},{4,14},{6,16},{8,18},{10,20},{12,22},{14,24},{16,26}... | collective-permute-start | bytes 5384 | tf_op jit(solution)/shard_map/ppermute | solution.py:335
  649.2 20.3 %collective-permute-start.7 = (f32[2,224]{1,0:T(2,128)S(1)}, f32[2,224]{1,0:T(2,128)S(1)}, u32[]{:S(2)}, u32[]{:S(2)}) collective-permute-start(f32[2,224]{1,0:T(2,128)S(1)} %get-tuple-element.102), channel_id=1, source_target_pairs={{0,16},{2,18},{4,20},{6,22},{8,24},{10,26},{12,28},{14,30},{16,0},... | collective-permute-start | bytes 5384 | tf_op jit(solution)/shard_map/ppermute | solution.py:335
  652.5 23.0 %collective-permute-start.6 = (f32[2,224]{1,0:T(2,128)S(1)}, f32[2,224]{1,0:T(2,128)S(1)}, u32[]{:S(2)}, u32[]{:S(2)}) collective-permute-start(f32[2,224]{1,0:T(2,128)S(1)} %get-tuple-element.103), channel_id=1, source_target_pairs={{0,18},{2,20},{4,22},{6,24},{8,26},{10,28},{12,30},{14,0},{16,2},{... | collective-permute-start | bytes 5384 | tf_op jit(solution)/shard_map/ppermute | solution.py:335
  654.7 22.6 %collective-permute-start.5 = (f32[2,224]{1,0:T(2,128)S(1)}, f32[2,224]{1,0:T(2,128)S(1)}, u32[]{:S(2)}, u32[]{:S(2)}) collective-permute-start(f32[2,224]{1,0:T(2,128)S(1)} %get-tuple-element.104), channel_id=1, source_target_pairs={{0,20},{2,22},{4,24},{6,26},{8,28},{10,30},{12,0},{14,2},{16,4},{1... | collective-permute-start | bytes 5384 | tf_op jit(solution)/shard_map/ppermute | solution.py:335
  658.6 45.6 %collective-permute-start.4 = (f32[2,224]{1,0:T(2,128)S(1)}, f32[2,224]{1,0:T(2,128)S(1)}, u32[]{:S(2)}, u32[]{:S(2)}) collective-permute-start(f32[2,224]{1,0:T(2,128)S(1)} %get-tuple-element.105), channel_id=1, source_target_pairs={{0,22},{2,24},{4,26},{6,28},{8,30},{10,0},{12,2},{14,4},{16,6},{18... | collective-permute-start | bytes 5384 | tf_op jit(solution)/shard_map/ppermute | solution.py:335
  658.6 47.4 %collective-permute-start.3 = (f32[2,224]{1,0:T(2,128)S(1)}, f32[2,224]{1,0:T(2,128)S(1)}, u32[]{:S(2)}, u32[]{:S(2)}) collective-permute-start(f32[2,224]{1,0:T(2,128)S(1)} %get-tuple-element.106), channel_id=1, source_target_pairs={{0,24},{2,26},{4,28},{6,30},{8,0},{10,2},{12,4},{14,6},{16,8},{18,... | collective-permute-start | bytes 5384 | tf_op jit(solution)/shard_map/ppermute | solution.py:335
  669.5 36.7 %collective-permute-start.2 = (f32[2,224]{1,0:T(2,128)S(1)}, f32[2,224]{1,0:T(2,128)S(1)}, u32[]{:S(2)}, u32[]{:S(2)}) collective-permute-start(f32[2,224]{1,0:T(2,128)S(1)} %get-tuple-element.107), channel_id=1, source_target_pairs={{0,26},{2,28},{4,30},{6,0},{8,2},{10,4},{12,6},{14,8},{16,10},{18,... | collective-permute-start | bytes 5384 | tf_op jit(solution)/shard_map/ppermute | solution.py:335
  675.6 31.7 %collective-permute-start.1 = (f32[2,224]{1,0:T(2,128)S(1)}, f32[2,224]{1,0:T(2,128)S(1)}, u32[]{:S(2)}, u32[]{:S(2)}) collective-permute-start(f32[2,224]{1,0:T(2,128)S(1)} %get-tuple-element.108), channel_id=1, source_target_pairs={{0,28},{2,30},{4,0},{6,2},{8,4},{10,6},{12,8},{14,10},{16,12},{18,... | collective-permute-start | bytes 5384 | tf_op jit(solution)/shard_map/ppermute | solution.py:335
  677.3 30.9 %collective-permute-start = (f32[2,224]{1,0:T(2,128)S(1)}, f32[2,224]{1,0:T(2,128)S(1)}, u32[]{:S(2)}, u32[]{:S(2)}) collective-permute-start(f32[2,224]{1,0:T(2,128)S(1)} %get-tuple-element.109), channel_id=1, source_target_pairs={{0,30},{2,0},{4,2},{6,4},{8,6},{10,8},{12,10},{14,12},{16,14},{18,... | collective-permute-start | bytes 5384 | tf_op jit(solution)/shard_map/ppermute | solution.py:335
  706.2 16.0 %collective-permute-start.27 = (bf16[560,128]{1,0:T(8,128)(2,1)S(1)}, bf16[560,128]{1,0:T(8,128)(2,1)S(1)}, u32[]{:S(2)}, u32[]{:S(2)}) collective-permute-start(bf16[560,128]{1,0:T(8,128)(2,1)S(1)} %copy-done.7), channel_id=1, source_target_pairs={{0,26},{2,28},{4,30},{6,0},{8,2},{10,4},{12,6},{14,8},{16,10},{18,... | collective-permute-start | bytes 430088 | tf_op jit(solution)/shard_map/ppermute | solution.py:335
  718.9 18.2 %collective-permute-start.19 = (bf16[560,128]{1,0:T(8,128)(2,1)S(1)}, bf16[560,128]{1,0:T(8,128)(2,1)S(1)}, u32[]{:S(2)}, u32[]{:S(2)}) collective-permute-start(bf16[560,128]{1,0:T(8,128)(2,1)S(1)} %copy-done.3), channel_id=1, source_target_pairs={{0,10},{2,12},{4,14},{6,16},{8,18},{10,20},{12,22},{14,24},{16,26}... | collective-permute-start | bytes 430088 | tf_op jit(solution)/shard_map/ppermute | solution.py:335
  722.4 28.7 %collective-permute-start.16 = (bf16[560,128]{1,0:T(8,128)(2,1)S(1)}, bf16[560,128]{1,0:T(8,128)(2,1)S(1)}, u32[]{:S(2)}, u32[]{:S(2)}) collective-permute-start(bf16[560,128]{1,0:T(8,128)(2,1)S(1)} %get-tuple-element.86), channel_id=1, source_target_pairs={{0,4},{2,6},{4,8},{6,10},{8,12},{10,14},{12,16},{14,18},{16,20},{1... | collective-permute-start | bytes 430088 | tf_op jit(solution)/shard_map/ppermute | solution.py:335
  733.5 23.0 %collective-permute-start.15 = (bf16[560,128]{1,0:T(8,128)(2,1)S(1)}, bf16[560,128]{1,0:T(8,128)(2,1)S(1)}, u32[]{:S(2)}, u32[]{:S(2)}) collective-permute-start(bf16[560,128]{1,0:T(8,128)(2,1)S(1)} %get-tuple-element.87), channel_id=1, source_target_pairs={{0,2},{2,4},{4,6},{6,8},{8,10},{10,12},{12,14},{14,16},{16,18},{18... | collective-permute-start | bytes 430088 | tf_op jit(solution)/shard_map/ppermute | solution.py:335
  737.1 19.4 %collective-permute-start.22 = (bf16[560,128]{1,0:T(8,128)(2,1)S(1)}, bf16[560,128]{1,0:T(8,128)(2,1)S(1)}, u32[]{:S(2)}, u32[]{:S(2)}) collective-permute-start(bf16[560,128]{1,0:T(8,128)(2,1)S(1)} %get-tuple-element.90), channel_id=1, source_target_pairs={{0,16},{2,18},{4,20},{6,22},{8,24},{10,26},{12,28},{14,30},{16,0},... | collective-permute-start | bytes 430088 | tf_op jit(solution)/shard_map/ppermute | solution.py:335
  737.1 19.4 %collective-permute-start.21 = (bf16[560,128]{1,0:T(8,128)(2,1)S(1)}, bf16[560,128]{1,0:T(8,128)(2,1)S(1)}, u32[]{:S(2)}, u32[]{:S(2)}) collective-permute-start(bf16[560,128]{1,0:T(8,128)(2,1)S(1)} %get-tuple-element.91), channel_id=1, source_target_pairs={{0,14},{2,16},{4,18},{6,20},{8,22},{10,24},{12,26},{14,28},{16,30}... | collective-permute-start | bytes 430088 | tf_op jit(solution)/shard_map/ppermute | solution.py:335
  737.4 19.1 %collective-permute-start.23 = (bf16[560,128]{1,0:T(8,128)(2,1)S(1)}, bf16[560,128]{1,0:T(8,128)(2,1)S(1)}, u32[]{:S(2)}, u32[]{:S(2)}) collective-permute-start(bf16[560,128]{1,0:T(8,128)(2,1)S(1)} %get-tuple-element.88), channel_id=1, source_target_pairs={{0,18},{2,20},{4,22},{6,24},{8,26},{10,28},{12,30},{14,0},{16,2},{... | collective-permute-start | bytes 430088 | tf_op jit(solution)/shard_map/ppermute | solution.py:335
  (22 other events, 1168.8 us)

commit v3 on v2

--- a/solution.py
+++ b/solution.py
@@ -164,7 +164,7 @@
     )(*tensors, *extras)
 
 
-def pack_rows_kernel(rows, width, extra, in_ref, extra_ref, out_ref):
+def pack_rows_pair(rows, width, extra, in_ref, out_ref, *refs):
     full, half = width // LANES, rows // 2
     slab = slab_of(half, 80)
     for side in range(2):
@@ -177,7 +177,7 @@
         def step(index, carry):
             lasts = []
             for part in range(2):
-                low = pl.multiple_of(part * half + index * slab, SLAB)
+                low = part * half + index * slab
                 values = [
                     in_ref[pl.ds(low, slab), tile * LANES : (tile + 1) * LANES].astype(jnp.float32)
                     for tile in range(side * full, side * full + full + 1)
@@ -189,37 +189,50 @@
                     pieces += [(value, 0, LANES) for value in values[1:-1]]
                     pieces += [(values[-1], 0, LANES // 2)]
                     for tile, value in enumerate(assemble(pieces)):
-                        to = pl.multiple_of(tile * rows + part * half + index * slab, SLAB)
+                        to = tile * rows + part * half + index * slab
                         out_ref[1, pl.ds(to, slab), :] = value.astype(jnp.bfloat16)
                     lasts.append((values[-1], LANES // 2, LANES // 2))
-            to = pl.multiple_of(full * rows + index * slab, SLAB)
+            to = full * rows + index * slab
             out_ref[side, pl.ds(to, slab), :] = assemble(lasts)[0].astype(jnp.bfloat16)
             return carry
 
-        lax.fori_loop(0, half // slab, step, 0)
+        for index in range(half // slab):
+            step(index, 0)
         if extra:
-            out_ref[side, pl.ds(tile_rows(rows, width), extra), :] = extra_ref[0]
-
-
-def pack_rows(count, tensor, extra):
+            out_ref[side, pl.ds(tile_rows(rows, width), extra), :] = refs[0][0]
+
+
+def pack_rows_kernel(rows, width, pairs, extra, in_ref, *refs):
+    for pair in range(pairs):
+        part = in_ref.at[:, pair * 2 * width : (pair + 1) * 2 * width]
+        pack_rows_pair(rows, width, extra, part, refs[-1].at[pl.ds(2 * pair, 2)], *refs[:-1])
+
+
+def pack_rows(count, tensor, extra=None):
     rows = tensor.shape[0]
     width = tensor.shape[1] // count
     body = tile_rows(rows, width)
-    extra_rows = extra.shape[1]
+    extras = [] if extra is None else [extra]
+    extra_rows = 0 if extra is None else extra.shape[1]
     if not rows_fit(count, rows, width):
         flat = tensor.reshape(rows, count, width).transpose(1, 0, 2).reshape(count, -1, LANES)
         return with_extra(count, flat, extra)
+    pairs = next(
+        pairs
+        for pairs in range(count // 2, 0, -1)
+        if count // 2 % pairs == 0 and (pairs == 1 or pairs * 4 * rows * width <= 2**19)
+    )
     return pl.pallas_call(
-        functools.partial(pack_rows_kernel, rows, width, extra_rows),
-        grid=(count // 2,),
+        functools.partial(pack_rows_kernel, rows, width, pairs, extra_rows),
+        grid=(count // 2 // pairs,),
         in_specs=[
-            pl.BlockSpec((rows, 2 * width), lambda f: (0, f)),
-            pl.BlockSpec((1, extra_rows, LANES), lambda f: (0, 0, 0)),
+            pl.BlockSpec((rows, 2 * pairs * width), lambda f: (0, f)),
+            *[pl.BlockSpec((1, extra_rows, LANES), lambda f: (0, 0, 0)) for _ in extras],
         ],
-        out_specs=pl.BlockSpec((2, body + extra_rows, LANES), lambda f: (f, 0, 0)),
+        out_specs=pl.BlockSpec((2 * pairs, body + extra_rows, LANES), lambda f: (f, 0, 0)),
         out_shape=jax.ShapeDtypeStruct((count, body + extra_rows, LANES), jnp.bfloat16),
         cost_estimate=cost(count * body * LANES),
-    )(tensor, extra)
+    )(tensor, *extras)
 
 
 def unpack_columns_kernel(widths, numbers, rows, factor_ref, in_ref, *out_refs):
@@ -341,11 +354,20 @@
     }
 
 
-def by_source(own, received):
+def by_source(own, received, stride=1):
+    places = lax.axis_size("fsdp") // stride
+    blocks = jnp.stack([received[stride * step] for step in range(places - 1, 0, -1)] + [own])
+    twice = jnp.concatenate([blocks, blocks])
+    return lax.dynamic_slice_in_dim(twice, places - 1 - lax.axis_index("fsdp") // stride, places)
+
+
+def from_all(own, received):
     count = lax.axis_size("fsdp")
-    blocks = jnp.stack([received[step] for step in range(count - 1, 0, -1)] + [own])
-    twice = jnp.concatenate([blocks, blocks])
-    return lax.dynamic_slice_in_dim(twice, count - 1 - lax.axis_index("fsdp"), count)
+    same = by_source(own, received, 2)
+    other = lax.ppermute(same, "fsdp", [(place, place ^ 1) for place in range(count)])
+    even = lax.axis_index("fsdp") % 2 == 0
+    pairs = jnp.stack([jnp.where(even, same, other), jnp.where(even, other, same)], axis=1)
+    return pairs.reshape((count,) + own.shape)
 
 
 def maxima_kernel(*refs):
@@ -447,8 +469,7 @@
     widths = [query_weight.shape[1], key_weight.shape[1], value_weight.shape[1]]
     group = query_weight.shape[1] // key_weight.shape[1]
 
-    sent_hidden = hidden.reshape(1, -1, LANES)
-    first = exchange(pack_rows(count, output_weight, sent_hidden))
+    first = exchange(pack_rows(count, output_weight))
     packed = pack_columns(count, trainer[:3])
 
     def block_of(blocks):
@@ -456,26 +477,28 @@
 
     received = {}
     steps = range(1, count)
-    bridges = [count // 2, count // 2 - 1, count // 2 + 1, count // 2 - 2]
+    bridges = [count // 2, count // 2 + 1, count // 2 - 2]
     received |= shifted(block_of(packed), [step for step in steps if step not in bridges])
     flat = [tensor.T for tensor in trainer]
     flat[3], flat[6] = output_weight, down_weight
     sent = pack_rows(count, down_weight, maxima(flat))
     second = exchange(sent, first)
     ready = after(packed, first)
-    received |= shifted(block_of(ready), bridges[:2])
+    received |= shifted(block_of(ready), bridges[:1])
+    slice_here = after(hidden.reshape(-1, LANES), first)
+    slices = shifted(lambda device: slice_here, range(2, count, 2))
+    slices = lax.optimization_barrier((slices, second))[0]
+    slices = from_all(slice_here, slices)
     sent = pack_columns(count, (after(up_weight, first),))
     third = exchange(sent, second)
     ready = after(packed, second)
-    received |= shifted(block_of(ready), bridges[2:])
+    received |= shifted(block_of(ready), bridges[1:])
 
     body = tile_rows(down_weight.shape[0], rows)
     heard = second[:, body:].reshape(count, -1)[:, :7].astype(jnp.float32)
     peaks = lax.pmax(jnp.max(heard, axis=0), "tp")
     factors, new_history = scaling(peaks, history, slot)
-    body = tile_rows(output_weight.shape[0], rows)
-    whole_hidden = first[:, body:].reshape(count, seqs, rows).transpose(1, 0, 2)
-    whole_hidden = whole_hidden.reshape(seqs, model)
+    whole_hidden = slices.reshape(count, seqs, rows).transpose(1, 0, 2).reshape(seqs, model)
     widened = whole_hidden.astype(jnp.float32)
     inv_rms = lax.rsqrt(jnp.mean(widened * widened, axis=1) + norm_eps)[:, None]
     fresh = jnp.concatenate(

time: 797 us -> 808 us (1.014)
  waiting for transfers between devices: 505 us -> 520 us
    ppermute x30 -> x37, waiting for transfers between devices: 154 us -> 191 us  [shifted(): lax.ppermute(block_for((here + step) % count), 'fsdp', [(place, (place +...]
    all_to_all x4, waiting for transfers between devices: 352 us -> 330 us  [exchange(): lax.all_to_all(after(blocks, *earlier), 'fsdp', split_axis=0, concat_axis...]
    ppermute x30 -> x37, starting transfers between devices: 60.5 us -> 65.6 us  [shifted(): lax.ppermute(block_for((here + step) % count), 'fsdp', [(place, (place +...]
    unnamed x62 -> x93, local copies, waits for them, and re-layouts: 25.3 us -> 25.3 us
  transfers between devices with their start and end apart: 34 -> 42, of which waited for: 5 -> 11; matrix products, arithmetic and copies ran while one was open for 10% -> 10% of each run, Pallas kernels for 13% -> 12%
where the time goes in v3:
time: 808 us; the launch traced here: 800 us
  waiting for transfers between devices  520 us (64%)
  Pallas kernels  108 us (13%)
  starting transfers between devices  87.9 us (11%)
  local copies, waits for them, and re-layouts  61.5 us (8%)
  matrix products  13.7 us (2%)
    all_to_all x4, waiting for transfers between devices, exchange(): lax.all_to_all(after(blocks, *earlier), 'fsdp', split_axis=0, concat_axis...  330 us
    ppermute x37, waiting for transfers between devices, shifted(): lax.ppermute(block_for((here + step) % count), 'fsdp', [(place, (place +...  191 us
    ppermute x37, starting transfers between devices, shifted(): lax.ppermute(block_for((here + step) % count), 'fsdp', [(place, (place +...  65.6 us
    pallas_call x3, Pallas kernels, pack_columns(): pl.pallas_call(functools.partial(pack_columns_kernel, widths, rows, extra...  36.4 us
    optimization_barrier x2, local copies, waits for them, and re-layouts, after(): return lax.optimization_barrier((tensor,) + earlier)[0]  25.4 us
    unnamed x93, local copies, waits for them, and re-layouts  25.3 us
    pallas_call x2, Pallas kernels, unpack_rows(): pl.pallas_call(functools.partial(unpack_rows_kernel, number, rows, width)...  23.4 us
    pallas_call x3, Pallas kernels, unpack_columns(): pl.pallas_call(functools.partial(unpack_columns_kernel, widths, numbers,...  21.6 us
  transfers between devices with their start and end apart: 42, of which 11 were waited for; matrix products, arithmetic and copies ran while one was open for 10% of the time, Pallas kernels for 12%

profile of v3, /device:TPU:13, one launch (start us, length us, event | category | flops | bytes accessed | tf_op | source)
XLA Modules:
  0.0 800.0 jit_solution(17340529788223421266)
XLA Ops:
  4.5 6.5 all-to-all-start
  11.0 12.3 %shard_map.197.refs_0_ = bf16[1,16,128]{2,1,0:T(8,128)(2,1)} custom-call(bf16[160,5120]{1,0:T(8,128)(2,1)} %bitcast.185, bf16[32,5120]{1,0:T(8,128)(2,1)} %bitcast.188, bf16[32,5120]{1,0:T(8,128)(2,1)} %bitcast.187, bf16[160,5120]{1,0:T(8,128)(2,1)} %refs_3_.1, bf16[864,5120]{1,0:T(8,128)(2,1)} %bitcast.184, bf16[864,5120]{1,0:T(8,128)(2,1)} %bitcast.183, ...), custom_call_target="tpu_custom_call" | custom-call | flops 7618560 | bytes 30474240 | tf_op jit(solution)/shard_map/pallas_call | solution.py:399
  23.3 10.1 %shard_map.198 = bf16[16,2176,128]{2,1,0:T(8,128)(2,1)} custom-call(bf16[864,5120]{1,0:T(8,128)(2,1)} %in_ref.3, bf16[1,16,128]{2,1,0:T(8,128)(2,1)} %shard_map.197.refs_0_), custom_call_target="tpu_custom_call" | custom-call | flops 4423680 | bytes 17694720 | tf_op jit(solution)/shard_map/pallas_call | solution.py:225
  33.4 15.2 %all-to-all-done.in_ref = bf16[16,400,128]{2,1,0:T(8,128)(2,1)S(1)} async-done(((bf16[16,400,128]{2,1,0:T(8,128)(2,1)}), bf16[16,400,128]{2,1,0:T(8,128)(2,1)S(1)}, u32[]{:S(2)}, u32[]{:S(2)}) %all-to-all-start) | async-done | bytes 1638432 | tf_op jit(solution)/shard_map/all_to_all | solution.py:55
  54.5 12.7 %copy.44.refs_0_ = bf16[5120,864]{1,0:T(8,128)(2,1)} copy(bf16[5120,864]{0,1:T(8,128)(2,1)} %param.19) | data formatting | bytes 17694720 | tf_op jit(solution)/shard_map/optimization_barrier | solution.py:51
  67.3 12.7 %shard_map.203 = bf16[16,2160,128]{2,1,0:T(8,128)(2,1)} custom-call(bf16[5120,864]{1,0:T(8,128)(2,1)} %copy.44.refs_0_), custom_call_target="tpu_custom_call" | custom-call | flops 4423680 | bytes 17694720 | tf_op jit(solution)/shard_map/pallas_call | solution.py:155
  80.0 168.2 %all-to-all-done.1.in_ref = bf16[16,2176,128]{2,1,0:T(8,128)(2,1)} async-done(((bf16[16,2176,128]{2,1,0:T(8,128)(2,1)}), bf16[16,2176,128]{2,1,0:T(8,128)(2,1)}, u32[]{:S(2)}, u32[]{:S(2)}) %all-to-all-start.1) | async-done | bytes 8912928 | tf_op jit(solution)/shard_map/all_to_all | solution.py:55
  248.1 4.8 all-to-all-start.2
  259.3 11.1 %shard_map.199 = bf16[16,560,128]{2,1,0:T(8,128)(2,1)} custom-call(bf16[5120,160]{1,0:T(8,128)(2,1)} %copy.40.refs_0_, bf16[5120,32]{1,0:T(8,128)(2,1)} %copy.41.refs_1_, bf16[5120,32]{1,0:T(8,128)(2,1)} %copy.42.refs_2_), custom_call_target="tpu_custom_call" | custom-call | flops 1146880 | bytes 4587520 | tf_op jit(solution)/shard_map/pallas_call | solution.py:155
  273.7 12.7 %copy.43.refs_0_ = bf16[5120,864]{1,0:T(8,128)(2,1)} copy(bf16[5120,864]{0,1:T(8,128)(2,1)} %param.18) | data formatting | bytes 17694720 | tf_op jit(solution)/shard_map/optimization_barrier | solution.py:51
  286.4 12.7 %shard_map.202 = bf16[16,2160,128]{2,1,0:T(8,128)(2,1)} custom-call(bf16[5120,864]{1,0:T(8,128)(2,1)} %copy.43.refs_0_), custom_call_target="tpu_custom_call" | custom-call | flops 4423680 | bytes 17694720 | tf_op jit(solution)/shard_map/pallas_call | solution.py:155
  299.1 146.4 %all-to-all-done.2.in_ref = bf16[16,2160,128]{2,1,0:T(8,128)(2,1)} async-done(((bf16[16,2160,128]{2,1,0:T(8,128)(2,1)}), bf16[16,2160,128]{2,1,0:T(8,128)(2,1)}, u32[]{:S(2)}, u32[]{:S(2)}) %all-to-all-start.2) | async-done | bytes 8847392 | tf_op jit(solution)/shard_map/all_to_all | solution.py:55
  445.5 5.2 all-to-all-start.3
  462.5 133.7 %collective-permute-done.4 = bf16[80,128]{1,0:T(8,128)(2,1)S(1)} collective-permute-done((bf16[80,128]{1,0:T(8,128)(2,1)S(1)}, bf16[80,128]{1,0:T(8,128)(2,1)S(1)}, u32[]{:S(2)}, u32[]{:S(2)}) %collective-permute-start.4) | collective-permute-done | bytes 20512 | tf_op jit(solution)/shard_map/ppermute | solution.py:348
  596.2 46.0 %collective-permute-done.3 = bf16[80,128]{1,0:T(8,128)(2,1)S(1)} collective-permute-done((bf16[80,128]{1,0:T(8,128)(2,1)S(1)}, bf16[80,128]{1,0:T(8,128)(2,1)S(1)}, u32[]{:S(2)}, u32[]{:S(2)}) %collective-permute-start.3) | collective-permute-done | bytes 20512 | tf_op jit(solution)/shard_map/ppermute | solution.py:348
  670.1 9.8 %shard_map.201 = bf16[2560,320]{1,0:T(8,128)(2,1)} custom-call(f32[7]{0:T(128)} %copy-done.16, bf16[16,400,128]{2,1,0:T(8,128)(2,1)} %copy-done), custom_call_target="tpu_custom_call" | custom-call | flops 819200 | bytes 3276800 | tf_op jit(solution)/shard_map/pallas_call | solution.py:324
  689.4 13.5 %shard_map.206 = bf16[13824,320]{1,0:T(8,128)(2,1)} custom-call(f32[7]{0:T(128)} %copy-done.16, bf16[16,2176,128]{2,1,0:T(8,128)(2,1)} %all-to-all-done.1.in_ref), custom_call_target="tpu_custom_call" | custom-call | flops 4423680 | bytes 17694720 | tf_op jit(solution)/shard_map/pallas_call | solution.py:324
  703.0 13.1 %copy.46 = bf16[13824,320]{0,1:T(8,128)(2,1)} copy(bf16[13824,320]{1,0:T(8,128)(2,1)} %shard_map.206) | data formatting | bytes 17694720
  723.8 5.9 select_reduce_fusion
  736.4 13.9 %collective-permute-start.24 = (bf16[560,128]{1,0:T(8,128)(2,1)S(1)}, bf16[560,128]{1,0:T(8,128)(2,1)S(1)}, u32[]{:S(2)}, u32[]{:S(2)}) collective-permute-start(bf16[560,128]{1,0:T(8,128)(2,1)S(1)} %copy-done.5), channel_id=1, source_target_pairs={{0,4},{2,6},{4,8},{6,10},{8,12},{10,14},{12,16},{14,18},{16,20},{1... | collective-permute-start | bytes 430088 | tf_op jit(solution)/shard_map/ppermute | solution.py:348
  753.8 5.5 collective-permute-start.30
  765.0 6.1 collective-permute-done.30
  782.9 8.6 %shard_map.205 = bf16[320,13824]{1,0:T(8,128)(2,1)} custom-call(f32[7]{0:T(128)} %copy-done.16, bf16[16,2160,128]{2,1,0:T(8,128)(2,1)} %all-to-all-done.2.in_ref), custom_call_target="tpu_custom_call" | custom-call | flops 4423680 | bytes 17694720 | tf_op jit(solution)/shard_map/pallas_call | solution.py:295
  791.4 8.6 %shard_map.204 = bf16[320,13824]{1,0:T(8,128)(2,1)} custom-call(f32[7]{0:T(128)} %copy-done.16, bf16[16,2160,128]{2,1,0:T(8,128)(2,1)} %all-to-all-done.3.in_ref), custom_call_target="tpu_custom_call" | custom-call | flops 4423680 | bytes 17694720 | tf_op jit(solution)/shard_map/pallas_call | solution.py:295
  (234 shorter events, 102.4 us)
Async XLA Ops:
  4.5 44.1 %all-to-all-start = ((bf16[16,400,128]{2,1,0:T(8,128)(2,1)}), bf16[16,400,128]{2,1,0:T(8,128)(2,1)S(1)}, u32[]{:S(2)}, u32[]{:S(2)}) async-start(bf16[16,400,128]{2,1,0:T(8,128)(2,1)} %shard_map.196), calls=%async_computation | async-start | bytes 3276800 | tf_op jit(solution)/shard_map/all_to_all | solution.py:55
  49.8 198.4 %all-to-all-start.1 = ((bf16[16,2176,128]{2,1,0:T(8,128)(2,1)}), bf16[16,2176,128]{2,1,0:T(8,128)(2,1)}, u32[]{:S(2)}, u32[]{:S(2)}) async-start(bf16[16,2176,128]{2,1,0:T(8,128)(2,1)} %shard_map.198), calls=%async_computation.1 | async-start | bytes 17825792 | tf_op jit(solution)/shard_map/all_to_all | solution.py:55
  248.1 197.4 %all-to-all-start.2 = ((bf16[16,2160,128]{2,1,0:T(8,128)(2,1)}), bf16[16,2160,128]{2,1,0:T(8,128)(2,1)}, u32[]{:S(2)}, u32[]{:S(2)}) async-start(bf16[16,2160,128]{2,1,0:T(8,128)(2,1)} %shard_map.203), calls=%async_computation.2 | async-start | bytes 17694720 | tf_op jit(solution)/shard_map/all_to_all | solution.py:55
  273.3 183.8 %collective-permute-start.6 = (bf16[80,128]{1,0:T(8,128)(2,1)S(1)}, bf16[80,128]{1,0:T(8,128)(2,1)S(1)}, u32[]{:S(2)}, u32[]{:S(2)}) collective-permute-start(bf16[80,128]{1,0:T(8,128)(2,1)S(1)} %reshape.171), channel_id=1, source_target_pairs={{0,28},{2,30},{4,0},{6,2},{8,4},{10,6},{12,8},{14,10},{16,12},{18,... | collective-permute-start | bytes 61448 | tf_op jit(solution)/shard_map/ppermute | solution.py:348
  273.6 183.6 %collective-permute-start.5 = (bf16[80,128]{1,0:T(8,128)(2,1)S(1)}, bf16[80,128]{1,0:T(8,128)(2,1)S(1)}, u32[]{:S(2)}, u32[]{:S(2)}) collective-permute-start(bf16[80,128]{1,0:T(8,128)(2,1)S(1)} %reshape.171), channel_id=1, source_target_pairs={{0,24},{2,26},{4,28},{6,30},{8,0},{10,2},{12,4},{14,6},{16,8},{18,... | collective-permute-start | bytes 61448 | tf_op jit(solution)/shard_map/ppermute | solution.py:348
  445.5 345.9 %all-to-all-start.3 = ((bf16[16,2160,128]{2,1,0:T(8,128)(2,1)}), bf16[16,2160,128]{2,1,0:T(8,128)(2,1)}, u32[]{:S(2)}, u32[]{:S(2)}) async-start(bf16[16,2160,128]{2,1,0:T(8,128)(2,1)} %shard_map.202), calls=%async_computation.3 | async-start | bytes 17694720 | tf_op jit(solution)/shard_map/all_to_all | solution.py:55
  450.8 145.4 %collective-permute-start.4 = (bf16[80,128]{1,0:T(8,128)(2,1)S(1)}, bf16[80,128]{1,0:T(8,128)(2,1)S(1)}, u32[]{:S(2)}, u32[]{:S(2)}) collective-permute-start(bf16[80,128]{1,0:T(8,128)(2,1)S(1)} %reshape.171), channel_id=1, source_target_pairs={{0,20},{2,22},{4,24},{6,26},{8,28},{10,30},{12,0},{14,2},{16,4},{1... | collective-permute-start | bytes 61448 | tf_op jit(solution)/shard_map/ppermute | solution.py:348
  451.0 191.3 %collective-permute-start.3 = (bf16[80,128]{1,0:T(8,128)(2,1)S(1)}, bf16[80,128]{1,0:T(8,128)(2,1)S(1)}, u32[]{:S(2)}, u32[]{:S(2)}) collective-permute-start(bf16[80,128]{1,0:T(8,128)(2,1)S(1)} %reshape.171), channel_id=1, source_target_pairs={{0,16},{2,18},{4,20},{6,22},{8,24},{10,26},{12,28},{14,30},{16,0},... | collective-permute-start | bytes 61448 | tf_op jit(solution)/shard_map/ppermute | solution.py:348
  453.2 189.5 %collective-permute-start.2 = (bf16[80,128]{1,0:T(8,128)(2,1)S(1)}, bf16[80,128]{1,0:T(8,128)(2,1)S(1)}, u32[]{:S(2)}, u32[]{:S(2)}) collective-permute-start(bf16[80,128]{1,0:T(8,128)(2,1)S(1)} %reshape.171), channel_id=1, source_target_pairs={{0,12},{2,14},{4,16},{6,18},{8,20},{10,22},{12,24},{14,26},{16,28}... | collective-permute-start | bytes 61448 | tf_op jit(solution)/shard_map/ppermute | solution.py:348
  457.1 186.1 %collective-permute-start.1 = (bf16[80,128]{1,0:T(8,128)(2,1)S(1)}, bf16[80,128]{1,0:T(8,128)(2,1)S(1)}, u32[]{:S(2)}, u32[]{:S(2)}) collective-permute-start(bf16[80,128]{1,0:T(8,128)(2,1)S(1)} %reshape.171), channel_id=1, source_target_pairs={{0,8},{2,10},{4,12},{6,14},{8,16},{10,18},{12,20},{14,22},{16,24},... | collective-permute-start | bytes 61448 | tf_op jit(solution)/shard_map/ppermute | solution.py:348
  457.2 186.4 %collective-permute-start = (bf16[80,128]{1,0:T(8,128)(2,1)S(1)}, bf16[80,128]{1,0:T(8,128)(2,1)S(1)}, u32[]{:S(2)}, u32[]{:S(2)}) collective-permute-start(bf16[80,128]{1,0:T(8,128)(2,1)S(1)} %reshape.171), channel_id=1, source_target_pairs={{0,4},{2,6},{4,8},{6,10},{8,12},{10,14},{12,16},{14,18},{16,20},{1... | collective-permute-start | bytes 61448 | tf_op jit(solution)/shard_map/ppermute | solution.py:348
  662.2 17.7 %collective-permute-start.15 = (f32[2,224]{1,0:T(2,128)S(1)}, f32[2,224]{1,0:T(2,128)S(1)}, u32[]{:S(2)}, u32[]{:S(2)}) collective-permute-start(f32[2,224]{1,0:T(2,128)S(1)} %get-tuple-element.119), channel_id=1, source_target_pairs={{0,16},{2,18},{4,20},{6,22},{8,24},{10,26},{12,28},{14,30},{16,0},... | collective-permute-start | bytes 5384 | tf_op jit(solution)/shard_map/ppermute | solution.py:348
  663.1 24.1 %collective-permute-start.14 = (f32[2,224]{1,0:T(2,128)S(1)}, f32[2,224]{1,0:T(2,128)S(1)}, u32[]{:S(2)}, u32[]{:S(2)}) collective-permute-start(f32[2,224]{1,0:T(2,128)S(1)} %get-tuple-element.120), channel_id=1, source_target_pairs={{0,18},{2,20},{4,22},{6,24},{8,26},{10,28},{12,30},{14,0},{16,2},{... | collective-permute-start | bytes 5384 | tf_op jit(solution)/shard_map/ppermute | solution.py:348
  665.9 23.5 %collective-permute-start.13 = (f32[2,224]{1,0:T(2,128)S(1)}, f32[2,224]{1,0:T(2,128)S(1)}, u32[]{:S(2)}, u32[]{:S(2)}) collective-permute-start(f32[2,224]{1,0:T(2,128)S(1)} %get-tuple-element.121), channel_id=1, source_target_pairs={{0,20},{2,22},{4,24},{6,26},{8,28},{10,30},{12,0},{14,2},{16,4},{1... | collective-permute-start | bytes 5384 | tf_op jit(solution)/shard_map/ppermute | solution.py:348
  667.3 48.9 %collective-permute-start.12 = (f32[2,224]{1,0:T(2,128)S(1)}, f32[2,224]{1,0:T(2,128)S(1)}, u32[]{:S(2)}, u32[]{:S(2)}) collective-permute-start(f32[2,224]{1,0:T(2,128)S(1)} %get-tuple-element.122), channel_id=1, source_target_pairs={{0,22},{2,24},{4,26},{6,28},{8,30},{10,0},{12,2},{14,4},{16,6},{18... | collective-permute-start | bytes 5384 | tf_op jit(solution)/shard_map/ppermute | solution.py:348
  669.8 46.9 %collective-permute-start.11 = (f32[2,224]{1,0:T(2,128)S(1)}, f32[2,224]{1,0:T(2,128)S(1)}, u32[]{:S(2)}, u32[]{:S(2)}) collective-permute-start(f32[2,224]{1,0:T(2,128)S(1)} %get-tuple-element.123), channel_id=1, source_target_pairs={{0,24},{2,26},{4,28},{6,30},{8,0},{10,2},{12,4},{14,6},{16,8},{18,... | collective-permute-start | bytes 5384 | tf_op jit(solution)/shard_map/ppermute | solution.py:348
  679.9 37.7 %collective-permute-start.10 = (f32[2,224]{1,0:T(2,128)S(1)}, f32[2,224]{1,0:T(2,128)S(1)}, u32[]{:S(2)}, u32[]{:S(2)}) collective-permute-start(f32[2,224]{1,0:T(2,128)S(1)} %get-tuple-element.124), channel_id=1, source_target_pairs={{0,26},{2,28},{4,30},{6,0},{8,2},{10,4},{12,6},{14,8},{16,10},{18,... | collective-permute-start | bytes 5384 | tf_op jit(solution)/shard_map/ppermute | solution.py:348
  687.2 31.8 %collective-permute-start.9 = (f32[2,224]{1,0:T(2,128)S(1)}, f32[2,224]{1,0:T(2,128)S(1)}, u32[]{:S(2)}, u32[]{:S(2)}) collective-permute-start(f32[2,224]{1,0:T(2,128)S(1)} %get-tuple-element.125), channel_id=1, source_target_pairs={{0,28},{2,30},{4,0},{6,2},{8,4},{10,6},{12,8},{14,10},{16,12},{18,... | collective-permute-start | bytes 5384 | tf_op jit(solution)/shard_map/ppermute | solution.py:348
  689.4 29.7 %collective-permute-start.8 = (f32[2,224]{1,0:T(2,128)S(1)}, f32[2,224]{1,0:T(2,128)S(1)}, u32[]{:S(2)}, u32[]{:S(2)}) collective-permute-start(f32[2,224]{1,0:T(2,128)S(1)} %get-tuple-element.126), channel_id=1, source_target_pairs={{0,30},{2,0},{4,2},{6,4},{8,6},{10,8},{12,10},{14,12},{16,14},{18,... | collective-permute-start | bytes 5384 | tf_op jit(solution)/shard_map/ppermute | solution.py:348
  730.7 19.6 %collective-permute-start.29 = (bf16[560,128]{1,0:T(8,128)(2,1)S(1)}, bf16[560,128]{1,0:T(8,128)(2,1)S(1)}, u32[]{:S(2)}, u32[]{:S(2)}) collective-permute-start(bf16[560,128]{1,0:T(8,128)(2,1)S(1)} %copy-done.9), channel_id=1, source_target_pairs={{0,14},{2,16},{4,18},{6,20},{8,22},{10,24},{12,26},{14,28},{16,30}... | collective-permute-start | bytes 430088 | tf_op jit(solution)/shard_map/ppermute | solution.py:348
  732.6 21.2 %collective-permute-start.27 = (bf16[560,128]{1,0:T(8,128)(2,1)S(1)}, bf16[560,128]{1,0:T(8,128)(2,1)S(1)}, u32[]{:S(2)}, u32[]{:S(2)}) collective-permute-start(bf16[560,128]{1,0:T(8,128)(2,1)S(1)} %copy-done.8), channel_id=1, source_target_pairs={{0,10},{2,12},{4,14},{6,16},{8,18},{10,20},{12,22},{14,24},{16,26}... | collective-permute-start | bytes 430088 | tf_op jit(solution)/shard_map/ppermute | solution.py:348
  734.6 24.7 %collective-permute-start.26 = (bf16[560,128]{1,0:T(8,128)(2,1)S(1)}, bf16[560,128]{1,0:T(8,128)(2,1)S(1)}, u32[]{:S(2)}, u32[]{:S(2)}) collective-permute-start(bf16[560,128]{1,0:T(8,128)(2,1)S(1)} %copy-done.7), channel_id=1, source_target_pairs={{0,8},{2,10},{4,12},{6,14},{8,16},{10,18},{12,20},{14,22},{16,24},... | collective-permute-start | bytes 430088 | tf_op jit(solution)/shard_map/ppermute | solution.py:348
  734.6 24.7 %collective-permute-start.25 = (bf16[560,128]{1,0:T(8,128)(2,1)S(1)}, bf16[560,128]{1,0:T(8,128)(2,1)S(1)}, u32[]{:S(2)}, u32[]{:S(2)}) collective-permute-start(bf16[560,128]{1,0:T(8,128)(2,1)S(1)} %copy-done.6), channel_id=1, source_target_pairs={{0,6},{2,8},{4,10},{6,12},{8,14},{10,16},{12,18},{14,20},{16,22},{... | collective-permute-start | bytes 430088 | tf_op jit(solution)/shard_map/ppermute | solution.py:348
  736.4 28.6 %collective-permute-start.24 = (bf16[560,128]{1,0:T(8,128)(2,1)S(1)}, bf16[560,128]{1,0:T(8,128)(2,1)S(1)}, u32[]{:S(2)}, u32[]{:S(2)}) collective-permute-start(bf16[560,128]{1,0:T(8,128)(2,1)S(1)} %copy-done.5), channel_id=1, source_target_pairs={{0,4},{2,6},{4,8},{6,10},{8,12},{10,14},{12,16},{14,18},{16,20},{1... | collective-permute-start | bytes 430088 | tf_op jit(solution)/shard_map/ppermute | solution.py:348
  (38 other events, 1089.3 us)
